TPU v7x, 8 devices: a whole 2x2x1 slice. The times are simulated.
8 devices in a mesh: dp: 2 (over z, y), tp: 4 (over x, core).
Axes of the slice: x: 2, y: 2, z: 1, core: 2. Of those that a mesh axis runs over, the one named last changes fastest.
Arguments:
- hidden_in: bfloat16 [32, 512, 768], P('dp', 'tp'), parts along dimension 0
- ln1_gain: bfloat16 [768], replicated
- ln1_bias: bfloat16 [768], replicated
- w_q: bfloat16 [768, 768], P(None, 'tp')
- b_q: bfloat16 [768], P('tp')
- w_k: bfloat16 [768, 768], P(None, 'tp')
- w_v: bfloat16 [768, 768], P(None, 'tp')
- b_v: bfloat16 [768], P('tp')
- w_o: bfloat16 [768, 768], P('tp')
- b_o: bfloat16 [768], replicated
- ln2_gain: bfloat16 [768], replicated
- ln2_bias: bfloat16 [768], replicated
- w_fc1: bfloat16 [768, 3072], P(None, 'tp')
- b_fc1: bfloat16 [3072], P('tp')
- w_fc2: bfloat16 [3072, 768], P('tp')
- b_fc2: bfloat16 [768], replicated
- post_gain: bfloat16 [768], replicated
- post_bias: bfloat16 [768], replicated
- w_ck: bfloat16 [4, 768, 768], P(None, None, 'tp')
- w_cv: bfloat16 [4, 768, 768], P(None, None, 'tp')
- b_cv: bfloat16 [4, 768], P(None, 'tp')
Outputs:
- output 1: bfloat16 [32, 512, 768], P('dp', 'tp'), parts along dimension 0
- output 2: bfloat16 [4, 32, 512, 12, 64], P(None, 'dp', None, 'tp'), parts along dimension 1
- output 3: bfloat16 [4, 32, 512, 12, 64], P(None, 'dp', None, 'tp'), parts along dimension 1
There are 2 independent parts. A program takes and returns all parts, laid end to end along the dimension named above; an argument that names none is the same for every part.
All inputs are finite; a program needn't handle non-finite values.
Results may differ from a plain program's by a relative error of at most 0.0152507.
Values are sent between devices in bfloat16 or wider.
A program may use at most 1 GiB of HBM per device.

v0:
```python
import jax
import jax.numpy as jnp
from jax import lax
from jax.sharding import PartitionSpec as P

HEAD_DIM = 64
ATTN_SCALE = HEAD_DIM ** -0.25
LN_EPS = 1e-5


def layer_norm(values, ln_gain, ln_bias):
    centered = values.astype(jnp.float32)
    centered = centered - jnp.mean(centered, axis=-1, keepdims=True)
    row_var = jnp.mean(centered * centered, axis=-1, keepdims=True)
    normed = centered * lax.rsqrt(row_var + LN_EPS)
    return (normed * ln_gain.astype(jnp.float32) + ln_bias.astype(jnp.float32)).astype(jnp.bfloat16)


def device_body(hidden_loc, ln1_gain, ln1_bias, w_q, b_q, w_k, w_v, b_v, w_o, b_o, ln2_gain, ln2_bias, w_fc1, b_fc1, w_fc2, b_fc2, post_gain, post_bias, w_ck, w_cv, b_cv):
    model_width = hidden_loc.shape[2]
    local_heads = w_q.shape[1] // HEAD_DIM
    num_layers = w_ck.shape[0]
    head_shape = (model_width, local_heads, HEAD_DIM)
    normed1 = layer_norm(hidden_loc, ln1_gain, ln1_bias)
    normed1_all = lax.all_gather(normed1, "tp", axis=1, tiled=True)
    bias_q = b_q.astype(jnp.float32).reshape(local_heads, 1, HEAD_DIM)
    bias_v = b_v.astype(jnp.float32).reshape(local_heads, 1, HEAD_DIM)
    q_heads = ((jnp.einsum("bfd,dhe->bhfe", normed1_all, w_q.reshape(head_shape), preferred_element_type=jnp.float32) + bias_q) * ATTN_SCALE).astype(jnp.bfloat16)
    k_heads = (jnp.einsum("bfd,dhe->bhfe", normed1_all, w_k.reshape(head_shape), preferred_element_type=jnp.float32) * ATTN_SCALE).astype(jnp.bfloat16)
    v_heads = (jnp.einsum("bfd,dhe->bhfe", normed1_all, w_v.reshape(head_shape), preferred_element_type=jnp.float32) + bias_v).astype(jnp.bfloat16)
    scores = jnp.einsum("bhqe,bhke->bhqk", q_heads, k_heads, preferred_element_type=jnp.float32)
    attn_probs = jax.nn.softmax(scores, axis=-1).astype(jnp.bfloat16)
    attn_heads = jnp.einsum("bhqk,bhke->bhqe", attn_probs, v_heads, preferred_element_type=jnp.float32).astype(jnp.bfloat16)
    part_attn = jnp.einsum("bhfe,hed->bfd", attn_heads, w_o.reshape(local_heads, HEAD_DIM, model_width), preferred_element_type=jnp.float32).astype(jnp.bfloat16)
    attn_sum = lax.psum_scatter(part_attn, "tp", scatter_dimension=1, tiled=True)
    attn_out = (attn_sum.astype(jnp.float32) + b_o.astype(jnp.float32)).astype(jnp.bfloat16)
    resid_one = (hidden_loc.astype(jnp.float32) + attn_out.astype(jnp.float32)).astype(jnp.bfloat16)
    normed2 = layer_norm(resid_one, ln2_gain, ln2_bias)
    normed2_all = lax.all_gather(normed2, "tp", axis=1, tiled=True)
    hidden_act = jax.nn.gelu(jnp.einsum("bfd,dc->bfc", normed2_all, w_fc1, preferred_element_type=jnp.float32) + b_fc1.astype(jnp.float32), approximate=False).astype(jnp.bfloat16)
    part_mlp = jnp.einsum("bfc,cd->bfd", hidden_act, w_fc2, preferred_element_type=jnp.float32).astype(jnp.bfloat16)
    mlp_sum = lax.psum_scatter(part_mlp, "tp", scatter_dimension=1, tiled=True)
    mlp_out = (mlp_sum.astype(jnp.float32) + b_fc2.astype(jnp.float32)).astype(jnp.bfloat16)
    resid_two = (resid_one.astype(jnp.float32) + mlp_out.astype(jnp.float32)).astype(jnp.bfloat16)
    enc_loc = layer_norm(resid_two, post_gain, post_bias)
    enc_all = lax.all_gather(enc_loc, "tp", axis=1, tiled=True)
    cache_shape = (num_layers, enc_all.shape[0], enc_all.shape[1], local_heads, HEAD_DIM)
    k_cache = jnp.einsum("bfd,ldc->lbfc", enc_all, w_ck, preferred_element_type=jnp.float32).astype(jnp.bfloat16).reshape(cache_shape)
    v_cache = (jnp.einsum("bfd,ldc->lbfc", enc_all, w_cv, preferred_element_type=jnp.float32) + b_cv.astype(jnp.float32)[:, None, None, :]).astype(jnp.bfloat16).reshape(cache_shape)
    return enc_loc, k_cache, v_cache


def solution(mesh):
    in_specs = (P("dp", "tp", None), P(), P(), P(None, "tp"), P("tp"), P(None, "tp"), P(None, "tp"), P("tp"), P("tp", None), P(), P(), P(), P(None, "tp"), P("tp"), P("tp", None), P(), P(), P(), P(None, None, "tp"), P(None, None, "tp"), P(None, "tp"))
    out_specs = (P("dp", "tp", None), P(None, "dp", None, "tp", None), P(None, "dp", None, "tp", None))
    return jax.shard_map(device_body, mesh=mesh, in_specs=in_specs, out_specs=out_specs, check_vma=False)
```

profile of v0, /device:TPU:0, one launch (start us, length us, event | category | flops | bytes accessed | tf_op | source)
XLA Modules:
  0.0 705.8 jit_solution(9594504481832389580)
XLA Ops:
  7.3 2.5 convert_reduce_fusion.1
  9.7 3.0 fusion.39
  12.7 0.7 convert_element_type.122
  13.4 0.7 convert_element_type.123
  14.1 3.8 fusion.42
  18.0 0.6 reduce-scatter.3.cloned.1.call-start
  18.7 82.2 %all-gather.4.cloned.1.call-done = bf16[16,512,768]{2,1,0:T(8,128)(2,1)} async-done(((bf16[16,128,768]{2,1,0:T(8,128)(2,1)}), bf16[16,512,768]{2,1,0:T(8,128)(2,1)}) %all-gather.4.cloned.1.call-update) | async-done | bytes 12582928 | tf_op jit(solution)/shard_map/all_gather | solution.py:25
  100.9 11.6 %fusion.50 = bf16[16,3,512,64]{3,2,1,0:T(8,128)(2,1)} fusion(bf16[768,3,64,1]{0,2,1,3:T(8,128)(2,1)S(1)} %bitcast.76, bf16[16,512,768]{2,1,0:T(8,128)(2,1)} %all-gather.4.cloned.1.call-done), kind=kOutput, calls=%fused_computation.71 | convolution fusion | flops 2419064832 | bytes 16023552 | tf_op jit(solution)/shard_map/bfd,dhe->bhfe/dot_general | solution.py:29
  112.5 11.7 %fusion.51 = bf16[16,3,512,64]{3,2,1,0:T(8,128)(2,1)} fusion(f32[3,64]{1,0:T(4,128)S(1)} %reshape.81, bf16[768,3,64,1]{0,2,1,3:T(8,128)(2,1)S(1)} %bitcast.77, bf16[16,512,768]{2,1,0:T(8,128)(2,1)S(1)} %copy-done.14), kind=kOutput, calls=%fused_computation.72 | convolution fusion | flops 2419064832 | bytes 16024320 | tf_op jit(solution)/shard_map/bfd,dhe->bhfe/dot_general | solution.py:30
  124.2 11.8 %fusion.49 = bf16[16,3,512,64]{3,2,1,0:T(8,128)(2,1)} fusion(f32[3,64]{1,0:T(4,128)S(1)} %reshape.80, bf16[768,3,64,1]{0,2,1,3:T(8,128)(2,1)S(1)} %bitcast.78, bf16[16,512,768]{2,1,0:T(8,128)(2,1)S(1)} %copy-done.14), kind=kOutput, calls=%fused_computation.70 | convolution fusion | flops 2420637696 | bytes 16024320 | tf_op jit(solution)/shard_map/bfd,dhe->bhfe/dot_general | solution.py:28
  136.0 54.2 %dot_general.40 = f32[16,3,512,64]{3,2,1,0:T(8,128)} custom-call(bf16[16,3,512,64]{3,2,1,0:T(8,128)(2,1)} %fusion.49, bf16[16,3,512,64]{3,2,1,0:T(8,128)(2,1)} %fusion.50, bf16[16,3,512,64]{3,2,1,0:T(8,128)(2,1)} %fusion.51), custom_call_target="tpu_custom_call" | custom-call | flops 3221225472 | bytes 9437184 | tf_op jit(solution)/shard_map/bhqk,bhke->bhqe/dot_general | solution.py:33
  190.2 12.8 %bitcast_convert_fusion = bf16[16,512,768]{2,1,0:T(8,128)(2,1)} fusion(bf16[3,64,768,1]{2,1,0,3:T(8,128)(2,1)S(1)} %bitcast.75, f32[16,3,512,64]{3,2,1,0:T(8,128)} %dot_general.40), kind=kOutput, calls=%fused_computation.9 | convolution fusion | flops 2423783424 | bytes 19169280 | tf_op jit(solution)/shard_map/bhfe,hed->bfd/dot_general | solution.py:34
  203.2 0.6 copy-done.4
  203.8 90.0 %reduce-scatter.3.cloned.1.call-done = bf16[16,128,768]{2,1,0:T(8,128)(2,1)} async-done(((bf16[16,512,768]{2,1,0:T(8,128)(2,1)}), bf16[16,128,768]{2,1,0:T(8,128)(2,1)}) %reduce-scatter.3.cloned.1.call-update) | async-done | bytes 3145744 | tf_op jit(solution)/shard_map/reduce_scatter | solution.py:35
  293.8 4.0 convert_reduce_fusion
  297.9 1.1 fusion.35
  299.0 0.5 copy-done.2
  299.5 2.4 fusion.38
  302.1 80.0 %all-gather.6.cloned.1.call-done = bf16[16,512,768]{2,1,0:T(8,128)(2,1)} async-done(((bf16[16,128,768]{2,1,0:T(8,128)(2,1)}), bf16[16,512,768]{2,1,0:T(8,128)(2,1)}) %all-gather.6.cloned.1.call-update) | async-done | bytes 12582928 | tf_op jit(solution)/shard_map/all_gather | solution.py:39
  382.1 23.7 %fusion.20 = (u16[512,768]{1,0:T(8,128)(2,1)S(1)}, u16[512,768]{1,0:T(8,128)(2,1)S(1)}, f32[16,512,768]{2,1,0:T(8,128)}) fusion(f32[768]{0:T(1024)S(1)} %convert_element_type.143, bf16[16,512,768]{2,1,0:T(8,128)(2,1)} %all-gather.6.cloned.1.call-done, bf16[768,768]{1,0:T(8,128)(2,1)S(1)} %copy-done), kind=kOutput, calls=%fused_computation.38 | convolution fusion | flops 9750970368 | bytes 40504320 | tf_op jit(solution)/shard_map/bfd,dc->bfc/dot_general | solution.py:40
  405.9 69.5 %fusion.32 = bf16[16,512,768]{2,1,0:T(8,128)(2,1)} fusion(f32[16,512,768]{2,1,0:T(8,128)} %get-tuple-element.15, f32[768]{0:T(1024)S(1)} %convert_element_type.143, u16[512,768]{1,0:T(8,128)(2,1)S(1)} %get-tuple-element.10, u16[512,768]{1,0:T(8,128)(2,1)S(1)} %get-tuple-element.9, bf16[768,768]{1,0:T(8,128)(2,1)S(1)} %copy-done.15), kind=kOutput, calls=%fused_computation.55 | convolution fusion | flops 10116661248 | bytes 40504320 | tf_op jit(solution)/shard_map/bfc,cd->bfd/dot_general | solution.py:41
  475.4 0.3 all-gather.8.cloned.1.call-start
  475.7 0.3 copy-done.8
  476.1 90.1 %reduce-scatter.5.cloned.1.call-done = bf16[16,128,768]{2,1,0:T(8,128)(2,1)} async-done(((bf16[16,512,768]{2,1,0:T(8,128)(2,1)}), bf16[16,128,768]{2,1,0:T(8,128)(2,1)}) %reduce-scatter.5.cloned.1.call-update) | async-done | bytes 3145744 | tf_op jit(solution)/shard_map/reduce_scatter | solution.py:42
  566.2 4.0 convert_reduce_fusion.2
  570.2 1.1 fusion.43
  571.3 2.5 fusion.46
  573.8 80.1 %all-gather.8.cloned.1.call-done = bf16[16,512,768]{2,1,0:T(8,128)(2,1)} async-done(((bf16[16,128,768]{2,1,0:T(8,128)(2,1)}), bf16[16,512,768]{2,1,0:T(8,128)(2,1)}) %all-gather.8.cloned.1.call-update) | async-done | bytes 12582928 | tf_op jit(solution)/shard_map/all_gather | solution.py:46
  653.9 13.3 %add_convert_fusion = bf16[16,512,4,192]{1,3,2,0:T(8,128)(2,1)S(1)} fusion(f32[4,192]{1,0:T(4,128)S(1)} %convert_element_type.157, bf16[16,512,768]{2,1,0:T(8,128)(2,1)} %all-gather.8.cloned.1.call-done, bf16[4,768,192]{1,2,0:T(8,128)(2,1)} %param.40), kind=kOutput, calls=%fused_computation.10 | convolution fusion | flops 9676259328 | bytes 26348544 | tf_op jit(solution)/shard_map/bfd,ldc->lbfc/dot_general | solution.py:49
  667.3 5.2 copy.29
  672.5 21.4 %fusion.29 = bf16[16,512,4,192]{1,3,2,0:T(8,128)(2,1)S(1)} fusion(bf16[16,512,768]{2,1,0:T(8,128)(2,1)} %all-gather.8.cloned.1.call-done, bf16[4,768,192]{1,2,0:T(8,128)(2,1)S(1)} %copy-done.16), kind=kOutput, calls=%fused_computation.54 | convolution fusion | flops 9669967872 | bytes 26345472 | tf_op jit(solution)/shard_map/bfd,ldc->lbfc/dot_general | solution.py:48
  693.9 5.1 copy.28
  (61 shorter events, 0.6 us)
Async XLA Ops:
  7.2 374.9 %copy-start = (bf16[768,768]{1,0:T(8,128)(2,1)S(1)}, bf16[768,768]{1,0:T(8,128)(2,1)}, u32[]{:S(2)}) copy-start(bf16[768,768]{1,0:T(8,128)(2,1)} %param.33) | copy-start | bytes 3538948
  7.2 11.4 %copy-start.12 = (bf16[192]{0:T(256)(128)(2,1)S(1)}, bf16[192]{0:T(256)(128)(2,1)}, u32[]{:S(2)}) copy-start(bf16[192]{0:T(256)(128)(2,1)} %param.28) | copy-start | bytes 1156
  7.2 11.4 %copy-start.13 = (bf16[192]{0:T(256)(128)(2,1)S(1)}, bf16[192]{0:T(256)(128)(2,1)}, u32[]{:S(2)}) copy-start(bf16[192]{0:T(256)(128)(2,1)} %param.25) | copy-start | bytes 1156
  7.2 93.7 %copy-start.17 = (bf16[768,192]{0,1:T(8,128)(2,1)S(1)}, bf16[768,192]{0,1:T(8,128)(2,1)}, u32[]{:S(2)}) copy-start(bf16[768,192]{0,1:T(8,128)(2,1)} %param.26) | copy-start | bytes 884740
  7.2 93.7 %all-gather.4.cloned.1.call-start = ((), (), s32[]{:S(2)}) async-start(), calls=%async_computation.2 | async-start | bytes 15728640 | tf_op jit(solution)/shard_map/all_gather | solution.py:25
  18.0 275.9 %reduce-scatter.3.cloned.1.call-start = ((), (), s32[]{:S(2)}) async-start(), calls=%async_computation.3 | async-start | bytes 15728640 | tf_op jit(solution)/shard_map/reduce_scatter | solution.py:35
  100.9 11.6 %copy-start.14 = (bf16[16,512,768]{2,1,0:T(8,128)(2,1)S(1)}, bf16[16,512,768]{2,1,0:T(8,128)(2,1)}, u32[]{:S(2)}) copy-start(bf16[16,512,768]{2,1,0:T(8,128)(2,1)} %all-gather.4.cloned.1.call-done) | copy-start | bytes 37748740
  100.9 11.6 %copy-start.18 = (bf16[768,192]{0,1:T(8,128)(2,1)S(1)}, bf16[768,192]{0,1:T(8,128)(2,1)}, u32[]{:S(2)}) copy-start(bf16[768,192]{0,1:T(8,128)(2,1)} %param.27) | copy-start | bytes 884740
  112.5 11.7 %copy-start.19 = (bf16[768,192]{0,1:T(8,128)(2,1)S(1)}, bf16[768,192]{0,1:T(8,128)(2,1)}, u32[]{:S(2)}) copy-start(bf16[768,192]{0,1:T(8,128)(2,1)} %param.24) | copy-start | bytes 884740
  136.0 54.2 %copy-start.3 = (bf16[192,768]{1,0:T(8,128)(2,1)S(1)}, bf16[192,768]{1,0:T(8,128)(2,1)}, u32[]{:S(2)}) copy-start(bf16[192,768]{1,0:T(8,128)(2,1)} %param.29) | copy-start | bytes 884740
  203.1 0.7 copy-start.4
  203.1 0.7 copy-start.5
  203.1 0.7 copy-start.6
  203.1 98.9 %copy-start.7 = (bf16[768]{0:T(1024)(128)(2,1)S(1)}, bf16[768]{0:T(1024)(128)(2,1)}, u32[]{:S(2)}) copy-start(bf16[768]{0:T(1024)(128)(2,1)} %param.34) | copy-start | bytes 4612
  203.1 179.0 %all-gather.6.cloned.1.call-start = ((), (), s32[]{:S(2)}) async-start(), calls=%async_computation.4 | async-start | bytes 15728640 | tf_op jit(solution)/shard_map/all_gather | solution.py:39
  297.9 1.7 copy-start.2
  302.0 264.2 %reduce-scatter.5.cloned.1.call-start = ((), (), s32[]{:S(2)}) async-start(), calls=%async_computation.5 | async-start | bytes 15728640 | tf_op jit(solution)/shard_map/reduce_scatter | solution.py:42
  302.1 103.8 %copy-start.15 = (bf16[768,768]{1,0:T(8,128)(2,1)S(1)}, bf16[768,768]{1,0:T(8,128)(2,1)}, u32[]{:S(2)}) copy-start(bf16[768,768]{1,0:T(8,128)(2,1)} %param.35) | copy-start | bytes 3538948
  475.4 0.7 copy-start.8
  475.4 0.7 copy-start.9
  475.4 0.7 copy-start.10
  475.4 98.4 %copy-start.11 = (bf16[4,192]{1,0:T(4,128)(2,1)S(1)}, bf16[4,192]{1,0:T(4,128)(2,1)}, u32[]{:S(2)}) copy-start(bf16[4,192]{1,0:T(4,128)(2,1)} %param.41) | copy-start | bytes 4612
  475.4 178.5 %all-gather.8.cloned.1.call-start = ((), (), s32[]{:S(2)}) async-start(), calls=%async_computation.6 | async-start | bytes 15728640 | tf_op jit(solution)/shard_map/all_gather | solution.py:46
  667.3 5.2 copy-start.16
  693.9 5.1 copy-start.1
Sparse Core Ops, SparseCore 0:
  18.1 82.7 all-gather.3
  203.2 90.5 reduce-scatter.2
  302.1 79.9 all-gather.5
  475.6 90.5 reduce-scatter.4
  573.9 79.9 all-gather.7
where the time goes:
time: 710 us; the launch traced here: 706 us
  waiting for transfers between devices  423 us (60%)
  matrix products  176 us (25%)
  Pallas kernels  54.2 us (8%)
  other arithmetic  25.8 us (4%)
  between operations  14.3 us (2%)
  local copies, waits for them, and re-layouts  12 us (2%)
    reduce_scatter x1, waiting for transfers between devices, device_body(): mlp_sum = lax.psum_scatter(part_mlp, 'tp', scatter_dimension=1, tiled=True)  90.1 us
    reduce_scatter x1, waiting for transfers between devices, device_body(): lax.psum_scatter(part_attn, 'tp', scatter_dimension=1, tiled=True)  90 us
    all_gather x1, waiting for transfers between devices, device_body(): normed1_all = lax.all_gather(normed1, 'tp', axis=1, tiled=True)  82.2 us
    all_gather x1, waiting for transfers between devices, device_body(): enc_all = lax.all_gather(enc_loc, 'tp', axis=1, tiled=True)  80.1 us
    all_gather x1, waiting for transfers between devices, device_body(): normed2_all = lax.all_gather(normed2, 'tp', axis=1, tiled=True)  80 us
    dot_general x1, matrix products, device_body(): jnp.einsum('bfc,cd->bfd', hidden_act, w_fc2, preferred_element_type=jnp.f...  69.5 us
    dot_general x1, Pallas kernels, device_body(): jnp.einsum('bhqk,bhke->bhqe', attn_probs, v_heads, preferred_element_type...  54.2 us
    dot_general x1, matrix products, device_body(): jnp.einsum('bfd,dc->bfc', normed2_all, w_fc1, preferred_element_type=jnp....  23.7 us
  transfers between devices with their start and end apart: 5, of which 5 were waited for; matrix products, arithmetic and copies ran while one was open for 0% of the time, Pallas kernels for 0%

commit v1 on v0

v1 whole, which is shorter than its diff:
```python
import functools

import jax
import jax.numpy as jnp
from jax import lax
from jax.experimental import pallas as pl
from jax.experimental.pallas import tpu as pltpu
from jax.sharding import PartitionSpec as P

HEAD_DIM = 64
ATTN_SCALE = HEAD_DIM ** -0.25
LN_EPS = 1e-5
SQRT_HALF = 0.5 ** 0.5
MESH = pl.DeviceIdType.MESH
BF16, F32 = jnp.bfloat16, jnp.float32

CLIPS, FRAMES, WIDTH, HIDDEN = 16, 512, 768, 3072
LOC_FRAMES = FRAMES // 4
SHARED, ONLY = 4, 2
SLOTS = SHARED + ONLY
LAG = 2
LN_ROWS = 64
SEND_ORDER = ("q", "k", "v", 0, "o", 1, 2, "w1a", "w1b", "w2a", "w2b", 3, 4, 5)

NT = (((1,), (1,)), ((), ()))
NN = (((1,), (0,)), ((), ()))


def dot(lhs, rhs, dims=NN):
    return lax.dot_general(lhs, rhs, dims, preferred_element_type=F32)


def norm_rows(values, gain, bias):
    centered = values.astype(F32)
    centered = centered - jnp.mean(centered, axis=-1, keepdims=True)
    row_var = jnp.mean(centered * centered, axis=-1, keepdims=True)
    return (centered * lax.rsqrt(row_var + LN_EPS) * gain + bias).astype(BF16)


def only_clip(chip, core, slot):
    return 2 * SHARED + (2 * chip + core) * ONLY + slot


def clip_of(chip, core, slot):
    return only_clip(chip, core, slot) if slot < ONLY else core * SHARED + slot - ONLY


def rows_of(ref, start, count):
    return ref.at[pl.ds(pl.multiple_of(start, 16), count), :]


def encoder_kernel(x_hbm, wq_hbm, wk_hbm, wv_hbm, wo_hbm, w1_hbm, w2_hbm, rep_ref, loc_hbm, e_hbm,
                   xbuf, wq, wk, wv, wo, w1, w2, small, abuf, qbuf, ktbuf, vbuf, obuf, mbuf, gbuf, acc, bias,
                   x_send, x_recv, x_loc, w_send, w_recv, w_loc, s_send, s_recv, s_loc, e_send, e_recv, e_loc):
    group, tp = lax.axis_index("dp"), lax.axis_index("tp")
    chip, core = tp // 2, tp % 2
    other_chip, other_core = 1 - chip, 1 - core
    t_sib = 2 * chip + other_core
    t_far = 2 * other_chip + core
    t_diag = 2 * other_chip + other_core
    sib = {"dp": group, "tp": t_sib}
    far = {"dp": group, "tp": t_far}
    diag = {"dp": group, "tp": t_diag}
    side = {"dp": 1 - group, "tp": tp}

    def remote(src, dst, send, recv, device):
        return pltpu.make_async_remote_copy(src_ref=src, dst_ref=dst, send_sem=send, recv_sem=recv, device_id=device, device_id_type=MESH)

    def frames(slot, owner):
        return xbuf.at[slot, pl.ds(pl.multiple_of(owner * LOC_FRAMES, LOC_FRAMES), LOC_FRAMES), :]

    def x_copy(slot, link):
        device, there_chip, there_core = ((sib, chip, other_core), (far, other_chip, core), (diag, other_chip, other_core))[link]
        return remote(x_hbm.at[clip_of(there_chip, there_core, slot)], frames(slot, tp), x_send.at[slot, link], x_recv.at[slot, link], device)

    def x_local(slot):
        return pltpu.make_async_copy(x_hbm.at[clip_of(chip, core, slot)], frames(slot, tp), x_loc.at[slot])

    def x_wait(slot):
        pltpu.make_async_copy(x_hbm.at[0], frames(slot, tp), x_loc.at[slot]).wait()
        for link, owner in enumerate((t_sib, t_far, t_diag)):
            remote(x_hbm.at[0], frames(slot, owner), x_send.at[slot, link], x_recv.at[slot, link], sib).wait_recv()

    units = {
        "q": (0, wq_hbm, wq, 192, 0, 192), "k": (1, wk_hbm, wk, 192, 0, 192), "v": (2, wv_hbm, wv, 192, 0, 192),
        "o": (3, wo_hbm, wo, 192, 0, 192),
        "w1a": (4, w1_hbm, w1, 768, 0, 384), "w1b": (5, w1_hbm, w1, 768, 384, 384),
        "w2a": (6, w2_hbm, w2, 768, 0, 384), "w2b": (7, w2_hbm, w2, 768, 384, 384),
    }

    def w_local(name):
        idx, src, dst, shard, first, count = units[name]
        return pltpu.make_async_copy(src.at[pl.ds(first, count), :], rows_of(dst, tp * shard + first, count), w_loc.at[idx])

    def w_sib(name, owner):
        idx, src, dst, shard, first, count = units[name]
        return remote(src.at[pl.ds(first, count), :], rows_of(dst, owner * shard + first, count), w_send.at[idx, 0], w_recv.at[idx, 0], sib)

    def w_far(name, owner):
        idx, src, dst, shard, first, count = units[name]
        half = count // 2
        return remote(rows_of(src, first + group * half, half), rows_of(dst, owner * shard + first + group * half, half),
                      w_send.at[idx, 1], w_recv.at[idx, 1], far)

    def w_relay(name, owner, part, sem, recv, device):
        idx, src, dst, shard, first, count = units[name]
        half = count // 2
        piece = rows_of(dst, owner * shard + first + part * half, half)
        return remote(piece, piece, w_send.at[idx, sem], w_recv.at[idx, recv], device)

    def w_start(name):
        w_far(name, tp).start()
        w_local(name).start()
        w_sib(name, tp).start()

    def w_stage1(name):
        w_far(name, t_far).wait_recv()
        w_relay(name, t_far, group, 3, 2, side).start()
        w_relay(name, t_far, group, 2, 3, sib).start()

    def w_stage2(name):
        w_relay(name, t_far, 1 - group, 3, 2, side).wait_recv()
        w_relay(name, t_far, 1 - group, 4, 4, sib).start()

    def w_wait_near(name):
        w_local(name).wait()
        w_sib(name, t_sib).wait_recv()

    def w_wait_far(name):
        w_relay(name, t_diag, group, 2, 3, sib).wait_recv()
        w_relay(name, t_diag, 1 - group, 4, 4, sib).wait_recv()

    def w_drain(name):
        w_sib(name, tp).wait_send()
        w_far(name, tp).wait_send()
        w_relay(name, t_far, group, 3, 2, side).wait_send()
        w_relay(name, t_far, group, 2, 3, sib).wait_send()
        w_relay(name, t_far, 1 - group, 4, 4, sib).wait_send()

    def s_copy(link, owner):
        device = (sib, far, diag)[link]
        return remote(loc_hbm, small.at[owner], s_send.at[link], s_recv.at[link], device)

    def e_local(slot, clip):
        return pltpu.make_async_copy(xbuf.at[slot], e_hbm.at[clip], e_loc.at[slot])

    def e_sib(slot, clip):
        return remote(xbuf.at[slot], e_hbm.at[clip], e_send.at[slot], e_recv.at[slot], sib)

    def e_far(slot, clip):
        return remote(xbuf.at[slot], e_hbm.at[clip], e_send.at[SLOTS + slot], e_recv.at[SLOTS + slot], far)

    def e_relay(slot, clip):
        sem = SLOTS + ONLY + slot
        return remote(e_hbm.at[clip], e_hbm.at[clip], e_send.at[sem], e_recv.at[sem], sib)

    barrier = pltpu.get_barrier_semaphore()
    for device in (sib, far, diag, side):
        pl.semaphore_signal(barrier, inc=1, device_id=device, device_id_type=MESH)
    pl.semaphore_wait(barrier, 4)

    small_local = pltpu.make_async_copy(loc_hbm, small.at[tp], s_loc)
    small_local.start()
    for link in range(3):
        s_copy(link, tp).start()
    for item in SEND_ORDER:
        if isinstance(item, str):
            w_start(item)
        else:
            x_copy(item, 1).start()
            x_copy(item, 2).start()
            x_local(item).start()
            x_copy(item, 0).start()

    small_local.wait()
    for link, owner in enumerate((t_sib, t_far, t_diag)):
        s_copy(link, owner).wait_recv()
    bias[0:1, :] = small[0, 1:2, :] + small[1, 1:2, :] + small[2, 1:2, :] + small[3, 1:2, :]
    bias[1:2, :] = small[0, 2:3, :] + small[1, 2:3, :] + small[2, 2:3, :] + small[3, 2:3, :]
    for name in ("q", "k", "v"):
        w_stage1(name)
    for name in ("q", "k", "v"):
        w_stage2(name)
    for name in ("q", "k", "v"):
        w_wait_near(name)
        w_wait_far(name)

    def rep(row):
        return rep_ref[row:row + 1, :]

    def norm_into(dst_store, src_load, gain, shift):
        for first in range(0, FRAMES, LN_ROWS):
            dst_store(first, norm_rows(src_load(first), gain, shift))

    def attention(slot, step):
        x_wait(slot)

        def put_a(first, value):
            abuf[first:first + LN_ROWS, :] = value

        norm_into(put_a, lambda first: xbuf[slot, pl.ds(first, LN_ROWS), :], rep(0), rep(1))
        for col in range(0, WIDTH, 256):
            cols = slice(col, col + 256)
            qbuf[:, cols] = ((dot(abuf[...], wq[cols, :], NT) + bias[0:1, cols]) * ATTN_SCALE).astype(BF16)
            vbuf[:, cols] = (dot(abuf[...], wv[cols, :], NT) + bias[1:2, cols]).astype(BF16)
            ktbuf[cols, :] = (dot(wk[cols, :], abuf[...], NT) * ATTN_SCALE).astype(BF16)

        lane = lax.broadcasted_iota(jnp.int32, (1, 128), 1)
        keep = [(lane < 64).astype(F32).astype(BF16), (lane >= 64).astype(F32).astype(BF16)]

        def pair_body(pair, _):
            cols = pl.ds(pl.multiple_of(pair * 128, 128), 128)
            keys_t = ktbuf[cols, :]
            values = vbuf[:, cols]
            parts = [(first, head) for first in (0, 256) for head in (0, 1)]

            def scores_of(part):
                first, head = part
                return dot(qbuf[first:first + 256, cols] * keep[head], keys_t)

            scores = scores_of(parts[0])
            outs = {}
            for index, part in enumerate(parts):
                ahead = scores_of(parts[index + 1]) if index + 1 < len(parts) else None
                top = jnp.max(scores, axis=-1, keepdims=True)
                weight = jnp.exp(scores - top)
                total = jnp.sum(weight, axis=-1, keepdims=True)
                outs[part] = dot(weight.astype(BF16), values) * (1.0 / total)
                scores = ahead
            for first in (0, 256):
                obuf[first:first + 256, cols] = jnp.where(lane < 64, outs[(first, 0)], outs[(first, 1)]).astype(BF16)
            return 0

        lax.fori_loop(0, 6, pair_body, 0)

        @pl.when(step == 0)
        def _():
            w_stage1("o")
            w_stage2("o")
            w_wait_near("o")
            w_wait_far("o")

        for col in range(0, WIDTH, 256):
            cols = slice(col, col + 256)
            branch = (dot(obuf[...], wo[:, cols]) + rep_ref[6:7, cols]).astype(BF16)
            xbuf[slot, :, cols] = (xbuf[slot, :, cols].astype(F32) + branch.astype(F32)).astype(BF16)

        def put_m(first, value):
            mbuf[slot, pl.ds(first, LN_ROWS), :] = value

        norm_into(put_m, lambda first: xbuf[slot, pl.ds(first, LN_ROWS), :], rep(2), rep(3))

    def hidden_half(slot, which):
        for half in range(2):
            shard = 2 * which + half
            for col in range(0, 768, 256):
                w1_part = w1[pl.ds(pl.multiple_of(shard * 768, 768), 768), col:col + 256]
                inner = dot(mbuf[slot], w1_part) + small[shard, 0:1, col:col + 256]
                gbuf[:, half * 768 + col:half * 768 + col + 256] = (0.5 * inner * (1.0 + lax.erf(inner * SQRT_HALF))).astype(BF16)

    def second_product(which, cols):
        return dot(gbuf[...], w2[pl.ds(pl.multiple_of(which * 1536, 1536), 1536), cols])

    def mlp_near(slot):
        hidden_half(slot, chip)
        for col in range(0, WIDTH, 256):
            cols = slice(col, col + 256)
            acc[slot, :, cols] = second_product(chip, cols)

    def mlp_far(slot):
        hidden_half(slot, other_chip)
        for col in range(0, WIDTH, 256):
            cols = slice(col, col + 256)
            branch = (acc[slot, :, cols] + second_product(other_chip, cols) + rep_ref[7:8, cols]).astype(BF16)
            xbuf[slot, :, cols] = (xbuf[slot, :, cols].astype(F32) + branch.astype(F32)).astype(BF16)

        def put_e(first, value):
            xbuf[slot, pl.ds(first, LN_ROWS), :] = value

        norm_into(put_e, lambda first: xbuf[slot, pl.ds(first, LN_ROWS), :], rep(4), rep(5))

        @pl.when(slot < ONLY)
        def _():
            clip = only_clip(chip, core, slot)
            e_far(slot, clip).start()
            e_local(slot, clip).start()
            e_sib(slot, clip).start()

        @pl.when(slot >= ONLY)
        def _():
            clip = core * SHARED + slot - ONLY
            e_local(slot, clip).start()
            e_sib(slot, clip).start()

    mlp_units = ("w1a", "w1b", "w2a", "w2b")

    def step_body(step, _):
        @pl.when(step < SLOTS)
        def _():
            attention(step, step)

        @pl.when(step == 0)
        def _():
            for name in mlp_units:
                w_wait_near(name)

        @pl.when(step < SLOTS)
        def _():
            mlp_near(step)

        @pl.when(step == LAG)
        def _():
            for name in mlp_units:
                w_stage1(name)
            for name in mlp_units:
                w_stage2(name)
            for name in mlp_units:
                w_wait_far(name)

        @pl.when(step >= LAG)
        def _():
            mlp_far(step - LAG)

        return 0

    lax.fori_loop(0, SLOTS + LAG, step_body, 0)

    for slot in range(ONLY):
        clip = only_clip(other_chip, core, slot)
        e_far(slot, clip).wait_recv()
        e_relay(slot, clip).start()
    for slot in range(SLOTS):
        clip = clip_of(chip, core, slot)
        e_local(slot, clip).wait()
        e_sib(slot, clip).wait_send()
        e_sib(slot, clip_of(chip, other_core, slot)).wait_recv()
    for slot in range(ONLY):
        e_far(slot, only_clip(chip, core, slot)).wait_send()
        e_relay(slot, only_clip(other_chip, core, slot)).wait_send()
        e_relay(slot, only_clip(other_chip, other_core, slot)).wait_recv()
    for slot in range(SLOTS):
        for link in range(3):
            x_copy(slot, link).wait_send()
    for name in units:
        w_drain(name)
    for link in range(3):
        s_copy(link, tp).wait_send()


def encode(x, wq_t, wk_t, wv_t, wo, w1, w2, rep, loc):
    dma = pltpu.SemaphoreType.DMA
    any_spec = pl.BlockSpec(memory_space=pl.ANY)
    return pl.pallas_call(
        encoder_kernel,
        out_shape=jax.ShapeDtypeStruct((CLIPS, FRAMES, WIDTH), BF16),
        in_specs=[any_spec] * 7 + [pl.BlockSpec(memory_space=pltpu.VMEM), any_spec],
        out_specs=any_spec,
        scratch_shapes=[
            pltpu.VMEM((SLOTS, FRAMES, WIDTH), BF16),
            pltpu.VMEM((WIDTH, WIDTH), BF16), pltpu.VMEM((WIDTH, WIDTH), BF16), pltpu.VMEM((WIDTH, WIDTH), BF16),
            pltpu.VMEM((WIDTH, WIDTH), BF16),
            pltpu.VMEM((HIDDEN, WIDTH), BF16), pltpu.VMEM((HIDDEN, WIDTH), BF16),
            pltpu.VMEM((4, 8, WIDTH), F32),
            pltpu.VMEM((FRAMES, WIDTH), BF16), pltpu.VMEM((FRAMES, WIDTH), BF16), pltpu.VMEM((WIDTH, FRAMES), BF16),
            pltpu.VMEM((FRAMES, WIDTH), BF16), pltpu.VMEM((FRAMES, WIDTH), BF16),
            pltpu.VMEM((SLOTS, FRAMES, WIDTH), BF16),
            pltpu.VMEM((FRAMES, 2 * WIDTH), BF16),
            pltpu.VMEM((SLOTS, FRAMES, WIDTH), F32),
            pltpu.VMEM((8, WIDTH), F32),
            dma((SLOTS, 3)), dma((SLOTS, 3)), dma((SLOTS,)),
            dma((8, 5)), dma((8, 5)), dma((8,)),
            dma((3,)), dma((3,)), dma,
            dma((SLOTS + 2 * ONLY,)), dma((SLOTS + 2 * ONLY,)), dma((SLOTS,)),
        ],
        compiler_params=pltpu.CompilerParams(collective_id=0, has_side_effects=True, vmem_limit_bytes=64 * 1024 * 1024 - 128 * 1024),
        name="encoder",
    )(x, wq_t, wk_t, wv_t, wo, w1, w2, rep, loc)


def cache_kernel(tp_ref, e_ref, wk_ref, wv_ref, bias_ref, k_ref, v_ref, enc_ref):
    enc_ref[0] = e_ref[0, pl.ds(pl.multiple_of(tp_ref[0] * LOC_FRAMES, LOC_FRAMES), LOC_FRAMES), :]
    for layer in range(4):
        k_ref[layer, 0] = dot(wk_ref[layer], e_ref[0], NT).astype(BF16)
        shift = jnp.concatenate([bias_ref[layer]] * 4, axis=1)
        v_ref[layer, 0] = (dot(wv_ref[layer], e_ref[0], NT) + shift).astype(BF16)


def caches(tp, e_all, wck_t, wcv_t, bias):
    cache = jax.ShapeDtypeStruct((4, CLIPS, 192, FRAMES), BF16)
    cache_spec = pl.BlockSpec((4, 1, 192, FRAMES), lambda clip, tp_ref: (0, clip, 0, 0))
    whole = lambda clip, tp_ref: (0, 0, 0)
    return pl.pallas_call(
        cache_kernel,
        out_shape=(cache, cache, jax.ShapeDtypeStruct((CLIPS, LOC_FRAMES, WIDTH), BF16)),
        grid_spec=pltpu.PrefetchScalarGridSpec(
            num_scalar_prefetch=1,
            grid=(CLIPS,),
            in_specs=[
                pl.BlockSpec((1, FRAMES, WIDTH), lambda clip, tp_ref: (clip, 0, 0)),
                pl.BlockSpec((4, 192, WIDTH), whole), pl.BlockSpec((4, 192, WIDTH), whole),
                pl.BlockSpec((4, 192, 128), whole),
            ],
            out_specs=(cache_spec, cache_spec, pl.BlockSpec((1, LOC_FRAMES, WIDTH), lambda clip, tp_ref: (clip, 0, 0))),
        ),
        compiler_params=pltpu.CompilerParams(dimension_semantics=("arbitrary",), vmem_limit_bytes=40 * 1024 * 1024),
        name="caches",
    )(tp, e_all, wck_t, wcv_t, bias)


def device_body(hidden_loc, ln1_gain, ln1_bias, w_q, b_q, w_k, w_v, b_v, w_o, b_o, ln2_gain, ln2_bias, w_fc1, b_fc1, w_fc2, b_fc2, post_gain, post_bias, w_ck, w_cv, b_cv):
    tp = lax.axis_index("tp")
    rep = jnp.stack([ln1_gain, ln1_bias, ln2_gain, ln2_bias, post_gain, post_bias, b_o, b_fc2]).astype(F32)
    mine = jnp.arange(WIDTH) // 192 == tp
    placed = lambda vec: jnp.where(mine, jnp.concatenate([vec] * 4), jnp.zeros((), BF16))
    zero = jnp.zeros((WIDTH,), BF16)
    loc = jnp.stack([b_fc1, placed(b_q), placed(b_v), zero, zero, zero, zero, zero]).astype(F32)
    e_all = encode(hidden_loc, w_q.T, w_k.T, w_v.T, w_o, w_fc1, w_fc2, rep, loc)
    bias = jnp.broadcast_to(b_cv.astype(F32)[:, :, None], (4, 192, 128))
    k_t, v_t, enc_loc = caches(tp.astype(jnp.int32).reshape(1), e_all, w_ck.transpose(0, 2, 1), w_cv.transpose(0, 2, 1), bias)
    shape = (4, CLIPS, FRAMES, 3, HEAD_DIM)
    return enc_loc, k_t.transpose(0, 1, 3, 2).reshape(shape), v_t.transpose(0, 1, 3, 2).reshape(shape)


def solution(mesh):
    in_specs = (P("dp", "tp", None), P(), P(), P(None, "tp"), P("tp"), P(None, "tp"), P(None, "tp"), P("tp"), P("tp", None), P(), P(), P(), P(None, "tp"), P("tp"), P("tp", None), P(), P(), P(), P(None, None, "tp"), P(None, None, "tp"), P(None, "tp"))
    out_specs = (P("dp", "tp", None), P(None, "dp", None, "tp", None), P(None, "dp", None, "tp", None))
    return jax.shard_map(device_body, mesh=mesh, in_specs=in_specs, out_specs=out_specs, check_vma=False)
```

time: 710 us -> 209 us (0.29)
  waiting for transfers between devices: 423 us -> 0 us
  matrix products: 176 us -> 0 us
  Pallas kernels: 54.2 us -> 193 us
  other arithmetic: 25.8 us -> 1.31 us
  between operations: 14.3 us -> 0.67 us
    all_gather x3 -> x0, waiting for transfers between devices: 242 us -> none  [the longest x1 82.2 us: device_body(): normed1_all = lax.all_gather(normed1, 'tp', axis=1, tiled=True)]
    pallas_call x0 -> x2, Pallas kernels: none -> 193 us  [the longest x1 156 us: encode(): pl.pallas_call(encoder_kernel, out_shape=jax.ShapeDtypeStruct((CLIPS, FRA...]
    reduce_scatter x2 -> x0, waiting for transfers between devices: 180 us -> none  [the longest x1 90.1 us: device_body(): mlp_sum = lax.psum_scatter(part_mlp, 'tp', scatter_dimension=1, tiled=True)]
    dot_general x8 -> x0, matrix products: 176 us -> none  [the longest x1 69.5 us: device_body(): jnp.einsum('bfc,cd->bfd', hidden_act, w_fc2, preferred_element_type=jnp.f...]
    dot_general x1 -> x0, Pallas kernels: 54.2 us -> none  [device_body(): jnp.einsum('bhqk,bhke->bhqe', attn_probs, v_heads, preferred_element_type...]
    reduce_sum x6 -> x0, other arithmetic: 15.7 us -> none  [the longest x3 10.5 us: layer_norm(): centered = centered - jnp.mean(centered, axis=-1, keepdims=True)]
    convert_element_type x13 -> x2, other arithmetic: 10.1 us -> 1.22 us  [the longest x1 0.61 us: device_body(): jnp.stack([b_fc1, placed(b_q), placed(b_v), zero, zero, zero, zero, zero])]
    unnamed x42 -> x6, local copies, waits for them, and re-layouts: 11.9 us -> 3.53 us
  transfers between devices with their start and end apart: 5 -> 0, of which waited for: 5 -> 0; matrix products, arithmetic and copies ran while one was open for 0% -> 0% of each run, Pallas kernels for 0% -> 0%
where the time goes in v1:
time: 209 us; the launch traced here: 208 us
  Pallas kernels  193 us (92%)
  local copies, waits for them, and re-layouts  12.7 us (6%)
    pallas_call x1, Pallas kernels, encode(): pl.pallas_call(encoder_kernel, out_shape=jax.ShapeDtypeStruct((CLIPS, FRA...  156 us
    pallas_call x1, Pallas kernels, caches(): pl.pallas_call(cache_kernel, out_shape=(cache, cache, jax.ShapeDtypeStruc...  37.5 us
    another operation x9, local copies, waits for them, and re-layouts, device_body(): jnp.stack([ln1_gain, ln1_bias, ln2_gain, ln2_bias, post_gain, post_bias,...  5.53 us

profile of v1, /device:TPU:0, one launch (start us, length us, event | category | flops | bytes accessed | tf_op | source)
XLA Modules:
  0.0 208.1 jit_solution(17392804036306785944)
XLA Ops:
  0.6 0.7 concatenate.24
  1.3 0.7 concatenate.26
  2.0 0.7 stack.38
  2.6 0.7 stack.39
  3.3 0.7 stack.44
  4.0 0.7 stack.40
  4.7 0.7 stack.41
  5.4 0.7 stack.47
  6.1 0.7 stack.45
  6.7 0.7 stack.42
  7.4 0.7 stack.43
  8.2 0.1 compare_select_fusion
  8.3 0.6 convert_element_type.10.loc_hbm
  8.9 0.6 convert_element_type.9.rep_ref
  9.5 1.6 broadcast_in_dim.12.bias_ref
  11.1 156.0 %encoder.1.e_ref = bf16[16,512,768]{2,1,0:T(8,128)(2,1)} custom-call(bf16[16,128,768]{2,1,0:T(8,128)(2,1)} %x_hbm.1, bf16[192,768]{1,0:T(8,128)(2,1)} %bitcast.14, bf16[192,768]{1,0:T(8,128)(2,1)} %bitcast.15, bf16[192,768]{1,0:T(8,128)(2,1)} %bitcast.16, bf16[192,768]{1,0:T(8,128)(2,1)} %wo_hbm.1, bf16[768,768]{1,0:T(8,128)(2,1)} %w1_hbm.1, ...), custom_call_target="tpu_custom_call" | custom-call | tf_op jit(solution)/shard_map/encoder/pallas_call | solution.py:353
  167.1 0.0 copy-start
  167.1 1.0 copy-done
  168.1 0.0 copy-start.1
  168.1 1.3 copy-done.1
  169.4 0.0 copy-start.2
  169.4 1.3 copy-done.2
  170.6 37.5 %caches.1 = (bf16[4,16,192,512]{3,2,1,0:T(8,128)(2,1)}, bf16[4,16,192,512]{3,2,1,0:T(8,128)(2,1)}, bf16[16,128,768]{2,1,0:T(8,128)(2,1)}) custom-call(s32[1]{0:T(128)} %bitcast.tp_ref, bf16[16,512,768]{2,1,0:T(8,128)(2,1)} %encoder.1.e_ref, bf16[4,192,768]{2,1,0:T(8,128)(2,1)S(1)} %bitcast.12, bf16[4,192,768]{2,1,0:T(8,128)(2,1)S(1)} %bitcast.13, ...), custom_call_target="tpu_custom_call" | custom-call | tf_op jit(solution)/shard_map/caches/pallas_call | solution.py:392
  (4 shorter events, 0.1 us)
Async XLA Ops:
  167.1 1.0 copy-start
  168.1 1.3 copy-start.1
  169.4 1.3 copy-start.2

commit v2 on v1

--- a/solution.py
+++ b/solution.py
@@ -18,12 +18,19 @@
 LOC_FRAMES = FRAMES // 4
 SHARED, ONLY = 4, 2
 SLOTS = SHARED + ONLY
-LAG = 2
+LAG = 5
 LN_ROWS = 64
-SEND_ORDER = ("q", "k", "v", 0, "o", 1, 2, "w1a", "w1b", "w2a", "w2b", 3, 4, 5)
+SEND_ORDER = ("q", "k", "v", 0, "o", 1, 2, 3, "w1a", "w1b", 4, "w2a", "w2b", 5)
+RELAYS = {
+    (4, 0): ((1, "w1a"), (1, "w1b")),
+    (5, 0): ((2, "w1a"), (2, "w1b")),
+    (5, 1): ((1, "w2a"), (1, "w2b")),
+    (5, 2): ((2, "w2a"), (2, "w2b")),
+}
 
 NT = (((1,), (1,)), ((), ()))
 NN = (((1,), (0,)), ((), ()))
+TN = (((0,), (0,)), ((), ()))
 
 
 def dot(lhs, rhs, dims=NN):
@@ -49,9 +56,10 @@
     return ref.at[pl.ds(pl.multiple_of(start, 16), count), :]
 
 
-def encoder_kernel(x_hbm, wq_hbm, wk_hbm, wv_hbm, wo_hbm, w1_hbm, w2_hbm, rep_ref, loc_hbm, e_hbm,
-                   xbuf, wq, wk, wv, wo, w1, w2, small, abuf, qbuf, ktbuf, vbuf, obuf, mbuf, gbuf, acc, bias,
-                   x_send, x_recv, x_loc, w_send, w_recv, w_loc, s_send, s_recv, s_loc, e_send, e_recv, e_loc):
+def encoder_kernel(x_hbm, wq_hbm, wk_hbm, wv_hbm, wo_hbm, w1_hbm, w2_hbm,
+                   g1_ref, s1_ref, g2_ref, s2_ref, g3_ref, s3_ref, bo_ref, b2_ref, b1_ref, bq_ref, bv_ref, e_hbm,
+                   rep_ref, loc, xbuf, wq, wk, wv, wo, w1, w2, small, abuf, qbuf, ktbuf, vbuf, obuf, mbuf, gbuf, acc, bias,
+                   x_send, x_recv, x_loc, w_send, w_recv, w_loc, s_send, s_recv, e_send, e_recv, e_loc):
     group, tp = lax.axis_index("dp"), lax.axis_index("tp")
     chip, core = tp // 2, tp % 2
     other_chip, other_core = 1 - chip, 1 - core
@@ -139,7 +147,7 @@
 
     def s_copy(link, owner):
         device = (sib, far, diag)[link]
-        return remote(loc_hbm, small.at[owner], s_send.at[link], s_recv.at[link], device)
+        return remote(loc, small.at[owner], s_send.at[link], s_recv.at[link], device)
 
     def e_local(slot, clip):
         return pltpu.make_async_copy(xbuf.at[slot], e_hbm.at[clip], e_loc.at[slot])
@@ -153,17 +161,27 @@
     def e_relay(slot, clip):
         sem = SLOTS + ONLY + slot
         return remote(e_hbm.at[clip], e_hbm.at[clip], e_send.at[sem], e_recv.at[sem], sib)
+
+    for row, ref in enumerate((g1_ref, s1_ref, g2_ref, s2_ref, g3_ref, s3_ref, bo_ref, b2_ref)):
+        rep_ref[row:row + 1, :] = ref[...].astype(F32).reshape(1, WIDTH)
+    place = lax.broadcasted_iota(jnp.int32, (192, WIDTH), 0) + tp * 192 == lax.broadcasted_iota(jnp.int32, (192, WIDTH), 1)
+    place = place.astype(F32).astype(BF16)
+    loc[0:1, :] = b1_ref[...].astype(F32).reshape(1, WIDTH)
+    for row, ref in ((1, bq_ref), (2, bv_ref)):
+        vector = jnp.broadcast_to(ref[...].astype(F32).reshape(1, 192), (16, 192)).astype(BF16)
+        loc[row:row + 1, :] = dot(vector, place)[0:1, :]
+    loc[3:8, :] = jnp.zeros((5, WIDTH), F32)
+    small[tp] = loc[...]
 
     barrier = pltpu.get_barrier_semaphore()
     for device in (sib, far, diag, side):
         pl.semaphore_signal(barrier, inc=1, device_id=device, device_id_type=MESH)
     pl.semaphore_wait(barrier, 4)
 
-    small_local = pltpu.make_async_copy(loc_hbm, small.at[tp], s_loc)
-    small_local.start()
-    for link in range(3):
-        s_copy(link, tp).start()
     for item in SEND_ORDER:
+        if item == 0:
+            for link in range(3):
+                s_copy(link, tp).start()
         if isinstance(item, str):
             w_start(item)
         else:
@@ -172,7 +190,6 @@
             x_local(item).start()
             x_copy(item, 0).start()
 
-    small_local.wait()
     for link, owner in enumerate((t_sib, t_far, t_diag)):
         s_copy(link, owner).wait_recv()
     bias[0:1, :] = small[0, 1:2, :] + small[1, 1:2, :] + small[2, 1:2, :] + small[3, 1:2, :]
@@ -294,10 +311,22 @@
 
     mlp_units = ("w1a", "w1b", "w2a", "w2b")
 
+    def relays(step, place):
+        for (when, where), todo in RELAYS.items():
+            if where == place:
+                @pl.when(step == when)
+                def _():
+                    for stage, name in todo:
+                        (w_stage1 if stage == 1 else w_stage2)(name)
+
     def step_body(step, _):
+        relays(step, 0)
+
         @pl.when(step < SLOTS)
         def _():
             attention(step, step)
+
+        relays(step, 1)
 
         @pl.when(step == 0)
         def _():
@@ -308,12 +337,10 @@
         def _():
             mlp_near(step)
 
+        relays(step, 2)
+
         @pl.when(step == LAG)
         def _():
-            for name in mlp_units:
-                w_stage1(name)
-            for name in mlp_units:
-                w_stage2(name)
             for name in mlp_units:
                 w_wait_far(name)
 
@@ -347,15 +374,16 @@
         s_copy(link, tp).wait_send()
 
 
-def encode(x, wq_t, wk_t, wv_t, wo, w1, w2, rep, loc):
+def encode(x, weights, vectors):
     dma = pltpu.SemaphoreType.DMA
     any_spec = pl.BlockSpec(memory_space=pl.ANY)
     return pl.pallas_call(
         encoder_kernel,
         out_shape=jax.ShapeDtypeStruct((CLIPS, FRAMES, WIDTH), BF16),
-        in_specs=[any_spec] * 7 + [pl.BlockSpec(memory_space=pltpu.VMEM), any_spec],
+        in_specs=[any_spec] * 7 + [pl.BlockSpec(memory_space=pltpu.VMEM)] * 11,
         out_specs=any_spec,
         scratch_shapes=[
+            pltpu.VMEM((8, WIDTH), F32), pltpu.VMEM((8, WIDTH), F32),
             pltpu.VMEM((SLOTS, FRAMES, WIDTH), BF16),
             pltpu.VMEM((WIDTH, WIDTH), BF16), pltpu.VMEM((WIDTH, WIDTH), BF16), pltpu.VMEM((WIDTH, WIDTH), BF16),
             pltpu.VMEM((WIDTH, WIDTH), BF16),
@@ -369,20 +397,30 @@
             pltpu.VMEM((8, WIDTH), F32),
             dma((SLOTS, 3)), dma((SLOTS, 3)), dma((SLOTS,)),
             dma((8, 5)), dma((8, 5)), dma((8,)),
-            dma((3,)), dma((3,)), dma,
+            dma((3,)), dma((3,)),
             dma((SLOTS + 2 * ONLY,)), dma((SLOTS + 2 * ONLY,)), dma((SLOTS,)),
         ],
         compiler_params=pltpu.CompilerParams(collective_id=0, has_side_effects=True, vmem_limit_bytes=64 * 1024 * 1024 - 128 * 1024),
         name="encoder",
-    )(x, wq_t, wk_t, wv_t, wo, w1, w2, rep, loc)
-
-
-def cache_kernel(tp_ref, e_ref, wk_ref, wv_ref, bias_ref, k_ref, v_ref, enc_ref):
+    )(x, *weights, *vectors)
+
+
+def cache_kernel(tp_ref, e_ref, wk_ref, wv_ref, bias_ref, k_ref, v_ref, enc_ref, shift):
+    @pl.when(pl.program_id(0) == 0)
+    def _():
+        rows = jnp.concatenate([bias_ref[...].astype(F32), jnp.zeros((4, 192), F32)], axis=0)
+        for layer in range(4):
+            pick = (lax.broadcasted_iota(jnp.int32, (8, 128), 0) == layer).astype(F32)
+            shift[layer * 192:layer * 192 + 192, :] = dot(rows, pick, TN)
+
     enc_ref[0] = e_ref[0, pl.ds(pl.multiple_of(tp_ref[0] * LOC_FRAMES, LOC_FRAMES), LOC_FRAMES), :]
-    for layer in range(4):
-        k_ref[layer, 0] = dot(wk_ref[layer], e_ref[0], NT).astype(BF16)
-        shift = jnp.concatenate([bias_ref[layer]] * 4, axis=1)
-        v_ref[layer, 0] = (dot(wv_ref[layer], e_ref[0], NT) + shift).astype(BF16)
+    for first in range(0, FRAMES, 256):
+        frames = slice(first, first + 256)
+        keys = dot(wk_ref[...].reshape(WIDTH, WIDTH), e_ref[0, frames, :], NT).astype(BF16)
+        values = (dot(wv_ref[...].reshape(WIDTH, WIDTH), e_ref[0, frames, :], NT) + jnp.concatenate([shift[...]] * 2, axis=1)).astype(BF16)
+        for layer in range(4):
+            k_ref[layer, 0, :, frames] = keys[layer * 192:layer * 192 + 192, :]
+            v_ref[layer, 0, :, frames] = values[layer * 192:layer * 192 + 192, :]
 
 
 def caches(tp, e_all, wck_t, wcv_t, bias):
@@ -398,25 +436,22 @@
             in_specs=[
                 pl.BlockSpec((1, FRAMES, WIDTH), lambda clip, tp_ref: (clip, 0, 0)),
                 pl.BlockSpec((4, 192, WIDTH), whole), pl.BlockSpec((4, 192, WIDTH), whole),
-                pl.BlockSpec((4, 192, 128), whole),
+                pl.BlockSpec((4, 192), lambda clip, tp_ref: (0, 0)),
             ],
             out_specs=(cache_spec, cache_spec, pl.BlockSpec((1, LOC_FRAMES, WIDTH), lambda clip, tp_ref: (clip, 0, 0))),
+            scratch_shapes=[pltpu.VMEM((WIDTH, 128), F32)],
         ),
-        compiler_params=pltpu.CompilerParams(dimension_semantics=("arbitrary",), vmem_limit_bytes=40 * 1024 * 1024),
+        compiler_params=pltpu.CompilerParams(dimension_semantics=("arbitrary",), vmem_limit_bytes=64 * 1024 * 1024 - 128 * 1024),
         name="caches",
     )(tp, e_all, wck_t, wcv_t, bias)
 
 
 def device_body(hidden_loc, ln1_gain, ln1_bias, w_q, b_q, w_k, w_v, b_v, w_o, b_o, ln2_gain, ln2_bias, w_fc1, b_fc1, w_fc2, b_fc2, post_gain, post_bias, w_ck, w_cv, b_cv):
-    tp = lax.axis_index("tp")
-    rep = jnp.stack([ln1_gain, ln1_bias, ln2_gain, ln2_bias, post_gain, post_bias, b_o, b_fc2]).astype(F32)
-    mine = jnp.arange(WIDTH) // 192 == tp
-    placed = lambda vec: jnp.where(mine, jnp.concatenate([vec] * 4), jnp.zeros((), BF16))
-    zero = jnp.zeros((WIDTH,), BF16)
-    loc = jnp.stack([b_fc1, placed(b_q), placed(b_v), zero, zero, zero, zero, zero]).astype(F32)
-    e_all = encode(hidden_loc, w_q.T, w_k.T, w_v.T, w_o, w_fc1, w_fc2, rep, loc)
-    bias = jnp.broadcast_to(b_cv.astype(F32)[:, :, None], (4, 192, 128))
-    k_t, v_t, enc_loc = caches(tp.astype(jnp.int32).reshape(1), e_all, w_ck.transpose(0, 2, 1), w_cv.transpose(0, 2, 1), bias)
+    weights = (w_q.T, w_k.T, w_v.T, w_o, w_fc1, w_fc2)
+    vectors = (ln1_gain, ln1_bias, ln2_gain, ln2_bias, post_gain, post_bias, b_o, b_fc2, b_fc1, b_q, b_v)
+    e_all = encode(hidden_loc, weights, vectors)
+    tp = lax.axis_index("tp").astype(jnp.int32).reshape(1)
+    k_t, v_t, enc_loc = caches(tp, e_all, w_ck.transpose(0, 2, 1), w_cv.transpose(0, 2, 1), b_cv)
     shape = (4, CLIPS, FRAMES, 3, HEAD_DIM)
     return enc_loc, k_t.transpose(0, 1, 3, 2).reshape(shape), v_t.transpose(0, 1, 3, 2).reshape(shape)
 

time: 209 us -> 195 us (0.933)
  local copies, waits for them, and re-layouts: 12.7 us -> 0 us
    pallas_call x1, Pallas kernels: 156 us -> 165 us  [encode(): pl.pallas_call(encoder_kernel, out_shape=jax.ShapeDtypeStruct((CLIPS, FRA...]
    pallas_call x1, Pallas kernels: 37.5 us -> 28.7 us  [caches(): pl.pallas_call(cache_kernel, out_shape=(cache, cache, jax.ShapeDtypeStruc...]
    another operation x12 -> x0, local copies, waits for them, and re-layouts: 6.25 us -> none  [the longest x9 5.53 us: device_body(): jnp.stack([ln1_gain, ln1_bias, ln2_gain, ln2_bias, post_gain, post_bias,...]
    unnamed x6 -> x0, local copies, waits for them, and re-layouts: 3.53 us -> none
where the time goes in v2:
time: 195 us
  Pallas kernels  194 us (99%)
    pallas_call x1, Pallas kernels, encode(): pl.pallas_call(encoder_kernel, out_shape=jax.ShapeDtypeStruct((CLIPS, FRA...  165 us
    pallas_call x1, Pallas kernels, caches(): pl.pallas_call(cache_kernel, out_shape=(cache, cache, jax.ShapeDtypeStruc...  28.7 us

profile of v2, /device:TPU:0, one launch (start us, length us, event | category | flops | bytes accessed | tf_op | source)
XLA Modules:
  0.0 194.7 jit_solution(10157230917991719339)
XLA Ops:
  0.6 165.4 %encoder.1.e_ref = bf16[16,512,768]{2,1,0:T(8,128)(2,1)} custom-call(bf16[16,128,768]{2,1,0:T(8,128)(2,1)} %x_hbm.1, bf16[192,768]{1,0:T(8,128)(2,1)} %bitcast.14, bf16[192,768]{1,0:T(8,128)(2,1)} %bitcast.15, bf16[192,768]{1,0:T(8,128)(2,1)} %bitcast.16, bf16[192,768]{1,0:T(8,128)(2,1)} %wo_hbm.1, bf16[768,768]{1,0:T(8,128)(2,1)} %w1_hbm.1, ...), custom_call_target="tpu_custom_call" | custom-call | tf_op jit(solution)/shard_map/encoder/pallas_call | solution.py:380
  166.0 28.7 %caches.1 = (bf16[4,16,192,512]{3,2,1,0:T(8,128)(2,1)}, bf16[4,16,192,512]{3,2,1,0:T(8,128)(2,1)}, bf16[16,128,768]{2,1,0:T(8,128)(2,1)}) custom-call(s32[1]{0:T(128)} %bitcast.tp_ref, bf16[16,512,768]{2,1,0:T(8,128)(2,1)} %encoder.1.e_ref, bf16[4,192,768]{2,1,0:T(8,128)(2,1)} %bitcast.12, bf16[4,192,768]{2,1,0:T(8,128)(2,1)} %bitcast.13, ...), custom_call_target="tpu_custom_call" | custom-call | tf_op jit(solution)/shard_map/caches/pallas_call | solution.py:430

commit v3 on v2

--- a/solution.py
+++ b/solution.py
@@ -15,17 +15,17 @@
 BF16, F32 = jnp.bfloat16, jnp.float32
 
 CLIPS, FRAMES, WIDTH, HIDDEN = 16, 512, 768, 3072
-LOC_FRAMES = FRAMES // 4
+LOC_FRAMES, LOC_COLS = FRAMES // 4, WIDTH // 4
+WIDE = (slice(0, 512), slice(512, 768))
 SHARED, ONLY = 4, 2
 SLOTS = SHARED + ONLY
-LAG = 5
+LAG = 3
 LN_ROWS = 64
-SEND_ORDER = ("q", "k", "v", 0, "o", 1, 2, 3, "w1a", "w1b", 4, "w2a", "w2b", 5)
+SEND_ORDER = ("q", "k", "v", 0, "o", 1, 2, "w1a", "w1b", 3, "w2a", "w2b", 4, 5)
 RELAYS = {
-    (4, 0): ((1, "w1a"), (1, "w1b")),
-    (5, 0): ((2, "w1a"), (2, "w1b")),
-    (5, 1): ((1, "w2a"), (1, "w2b")),
-    (5, 2): ((2, "w2a"), (2, "w2b")),
+    (3, 0): ((1, "w1a"), (1, "w1b")),
+    (3, 1): ((2, "w1a"), (2, "w1b"), (1, "w2a"), (1, "w2b")),
+    (3, 2): ((2, "w2a"), (2, "w2b")),
 }
 
 NT = (((1,), (1,)), ((), ()))
@@ -58,7 +58,7 @@
 
 def encoder_kernel(x_hbm, wq_hbm, wk_hbm, wv_hbm, wo_hbm, w1_hbm, w2_hbm,
                    g1_ref, s1_ref, g2_ref, s2_ref, g3_ref, s3_ref, bo_ref, b2_ref, b1_ref, bq_ref, bv_ref, e_hbm,
-                   rep_ref, loc, xbuf, wq, wk, wv, wo, w1, w2, small, abuf, qbuf, ktbuf, vbuf, obuf, mbuf, gbuf, acc, bias,
+                   rep_ref, loc, b1_row, xbuf, wqv, wk, wo, w1, w2, small, abuf, qvbuf, ktbuf, obuf, mbuf, gbuf, acc, bias,
                    x_send, x_recv, x_loc, w_send, w_recv, w_loc, s_send, s_recv, e_send, e_recv, e_loc):
     group, tp = lax.axis_index("dp"), lax.axis_index("tp")
     chip, core = tp // 2, tp % 2
@@ -89,31 +89,38 @@
         for link, owner in enumerate((t_sib, t_far, t_diag)):
             remote(x_hbm.at[0], frames(slot, owner), x_send.at[slot, link], x_recv.at[slot, link], sib).wait_recv()
 
+    def at_rows(dst, base):
+        shard = LOC_COLS if dst is not w2 else WIDTH
+        return lambda owner, first, count: rows_of(dst, base + owner * shard + first, count)
+
+    def at_columns(owner, first, count):
+        return w1.at[pl.ds(pl.multiple_of(first, 16), count), pl.ds(pl.multiple_of(owner * WIDTH, WIDTH), WIDTH)]
+
     units = {
-        "q": (0, wq_hbm, wq, 192, 0, 192), "k": (1, wk_hbm, wk, 192, 0, 192), "v": (2, wv_hbm, wv, 192, 0, 192),
-        "o": (3, wo_hbm, wo, 192, 0, 192),
-        "w1a": (4, w1_hbm, w1, 768, 0, 384), "w1b": (5, w1_hbm, w1, 768, 384, 384),
-        "w2a": (6, w2_hbm, w2, 768, 0, 384), "w2b": (7, w2_hbm, w2, 768, 384, 384),
+        "q": (0, wq_hbm, at_rows(wqv, 0), 0, 192), "k": (1, wk_hbm, at_rows(wk, 0), 0, 192),
+        "v": (2, wv_hbm, at_rows(wqv, WIDTH), 0, 192), "o": (3, wo_hbm, at_rows(wo, 0), 0, 192),
+        "w1a": (4, w1_hbm, at_columns, 0, 384), "w1b": (5, w1_hbm, at_columns, 384, 384),
+        "w2a": (6, w2_hbm, at_rows(w2, 0), 0, 384), "w2b": (7, w2_hbm, at_rows(w2, 0), 384, 384),
     }
 
     def w_local(name):
-        idx, src, dst, shard, first, count = units[name]
-        return pltpu.make_async_copy(src.at[pl.ds(first, count), :], rows_of(dst, tp * shard + first, count), w_loc.at[idx])
+        idx, src, place, first, count = units[name]
+        return pltpu.make_async_copy(src.at[pl.ds(first, count), :], place(tp, first, count), w_loc.at[idx])
 
     def w_sib(name, owner):
-        idx, src, dst, shard, first, count = units[name]
-        return remote(src.at[pl.ds(first, count), :], rows_of(dst, owner * shard + first, count), w_send.at[idx, 0], w_recv.at[idx, 0], sib)
+        idx, src, place, first, count = units[name]
+        return remote(src.at[pl.ds(first, count), :], place(owner, first, count), w_send.at[idx, 0], w_recv.at[idx, 0], sib)
 
     def w_far(name, owner):
-        idx, src, dst, shard, first, count = units[name]
+        idx, src, place, first, count = units[name]
         half = count // 2
-        return remote(rows_of(src, first + group * half, half), rows_of(dst, owner * shard + first + group * half, half),
+        return remote(rows_of(src, first + group * half, half), place(owner, first + group * half, half),
                       w_send.at[idx, 1], w_recv.at[idx, 1], far)
 
     def w_relay(name, owner, part, sem, recv, device):
-        idx, src, dst, shard, first, count = units[name]
+        idx, src, place, first, count = units[name]
         half = count // 2
-        piece = rows_of(dst, owner * shard + first + part * half, half)
+        piece = place(owner, first + part * half, half)
         return remote(piece, piece, w_send.at[idx, sem], w_recv.at[idx, recv], device)
 
     def w_start(name):
@@ -192,8 +199,10 @@
 
     for link, owner in enumerate((t_sib, t_far, t_diag)):
         s_copy(link, owner).wait_recv()
-    bias[0:1, :] = small[0, 1:2, :] + small[1, 1:2, :] + small[2, 1:2, :] + small[3, 1:2, :]
-    bias[1:2, :] = small[0, 2:3, :] + small[1, 2:3, :] + small[2, 2:3, :] + small[3, 2:3, :]
+    bias[0:1, 0:WIDTH] = small[0, 1:2, :] + small[1, 1:2, :] + small[2, 1:2, :] + small[3, 1:2, :]
+    bias[0:1, WIDTH:2 * WIDTH] = small[0, 2:3, :] + small[1, 2:3, :] + small[2, 2:3, :] + small[3, 2:3, :]
+    for owner in range(4):
+        b1_row[0:1, owner * WIDTH:owner * WIDTH + WIDTH] = small[owner, 0:1, :]
     for name in ("q", "k", "v"):
         w_stage1(name)
     for name in ("q", "k", "v"):
@@ -216,11 +225,11 @@
             abuf[first:first + LN_ROWS, :] = value
 
         norm_into(put_a, lambda first: xbuf[slot, pl.ds(first, LN_ROWS), :], rep(0), rep(1))
-        for col in range(0, WIDTH, 256):
-            cols = slice(col, col + 256)
-            qbuf[:, cols] = ((dot(abuf[...], wq[cols, :], NT) + bias[0:1, cols]) * ATTN_SCALE).astype(BF16)
-            vbuf[:, cols] = (dot(abuf[...], wv[cols, :], NT) + bias[1:2, cols]).astype(BF16)
-            ktbuf[cols, :] = (dot(wk[cols, :], abuf[...], NT) * ATTN_SCALE).astype(BF16)
+        scale = jnp.where(lax.broadcasted_iota(jnp.int32, (1, 2 * WIDTH), 1) < WIDTH, ATTN_SCALE, 1.0)
+        ktbuf[...] = (dot(wk[...], abuf[...], NT) * ATTN_SCALE).astype(BF16)
+        for col in range(0, 2 * WIDTH, 512):
+            cols = slice(col, col + 512)
+            qvbuf[:, cols] = ((dot(abuf[...], wqv[cols, :], NT) + bias[0:1, cols]) * scale[:, cols]).astype(BF16)
 
         lane = lax.broadcasted_iota(jnp.int32, (1, 128), 1)
         keep = [(lane < 64).astype(F32).astype(BF16), (lane >= 64).astype(F32).astype(BF16)]
@@ -228,24 +237,21 @@
         def pair_body(pair, _):
             cols = pl.ds(pl.multiple_of(pair * 128, 128), 128)
             keys_t = ktbuf[cols, :]
-            values = vbuf[:, cols]
-            parts = [(first, head) for first in (0, 256) for head in (0, 1)]
-
-            def scores_of(part):
-                first, head = part
-                return dot(qbuf[first:first + 256, cols] * keep[head], keys_t)
-
-            scores = scores_of(parts[0])
-            outs = {}
-            for index, part in enumerate(parts):
-                ahead = scores_of(parts[index + 1]) if index + 1 < len(parts) else None
+            values = qvbuf[:, pl.ds(pl.multiple_of(WIDTH + pair * 128, 128), 128)]
+
+            def scores_of(head):
+                return dot(qvbuf[:, cols] * keep[head], keys_t)
+
+            scores = scores_of(0)
+            outs = []
+            for head in range(2):
+                ahead = scores_of(1) if head == 0 else None
                 top = jnp.max(scores, axis=-1, keepdims=True)
                 weight = jnp.exp(scores - top)
                 total = jnp.sum(weight, axis=-1, keepdims=True)
-                outs[part] = dot(weight.astype(BF16), values) * (1.0 / total)
+                outs.append(dot(weight.astype(BF16), values) * (1.0 / total))
                 scores = ahead
-            for first in (0, 256):
-                obuf[first:first + 256, cols] = jnp.where(lane < 64, outs[(first, 0)], outs[(first, 1)]).astype(BF16)
+            obuf[:, cols] = jnp.where(lane < 64, outs[0], outs[1]).astype(BF16)
             return 0
 
         lax.fori_loop(0, 6, pair_body, 0)
@@ -257,8 +263,7 @@
             w_wait_near("o")
             w_wait_far("o")
 
-        for col in range(0, WIDTH, 256):
-            cols = slice(col, col + 256)
+        for cols in WIDE:
             branch = (dot(obuf[...], wo[:, cols]) + rep_ref[6:7, cols]).astype(BF16)
             xbuf[slot, :, cols] = (xbuf[slot, :, cols].astype(F32) + branch.astype(F32)).astype(BF16)
 
@@ -268,26 +273,27 @@
         norm_into(put_m, lambda first: xbuf[slot, pl.ds(first, LN_ROWS), :], rep(2), rep(3))
 
     def hidden_half(slot, which):
-        for half in range(2):
-            shard = 2 * which + half
-            for col in range(0, 768, 256):
-                w1_part = w1[pl.ds(pl.multiple_of(shard * 768, 768), 768), col:col + 256]
-                inner = dot(mbuf[slot], w1_part) + small[shard, 0:1, col:col + 256]
-                gbuf[:, half * 768 + col:half * 768 + col + 256] = (0.5 * inner * (1.0 + lax.erf(inner * SQRT_HALF))).astype(BF16)
+        def product(col):
+            return dot(mbuf[slot], w1[:, pl.ds(pl.multiple_of(which * 1536 + col, 512), 512)])
+
+        ahead = product(0)
+        for col in range(0, 1536, 512):
+            inner = ahead + b1_row[0:1, pl.ds(pl.multiple_of(which * 1536 + col, 512), 512)]
+            if col + 512 < 1536:
+                ahead = product(col + 512)
+            gbuf[:, col:col + 512] = (0.5 * inner * (1.0 + lax.erf(inner * SQRT_HALF))).astype(BF16)
 
     def second_product(which, cols):
         return dot(gbuf[...], w2[pl.ds(pl.multiple_of(which * 1536, 1536), 1536), cols])
 
     def mlp_near(slot):
         hidden_half(slot, chip)
-        for col in range(0, WIDTH, 256):
-            cols = slice(col, col + 256)
+        for cols in WIDE:
             acc[slot, :, cols] = second_product(chip, cols)
 
     def mlp_far(slot):
         hidden_half(slot, other_chip)
-        for col in range(0, WIDTH, 256):
-            cols = slice(col, col + 256)
+        for cols in WIDE:
             branch = (acc[slot, :, cols] + second_product(other_chip, cols) + rep_ref[7:8, cols]).astype(BF16)
             xbuf[slot, :, cols] = (xbuf[slot, :, cols].astype(F32) + branch.astype(F32)).astype(BF16)
 
@@ -383,18 +389,17 @@
         in_specs=[any_spec] * 7 + [pl.BlockSpec(memory_space=pltpu.VMEM)] * 11,
         out_specs=any_spec,
         scratch_shapes=[
-            pltpu.VMEM((8, WIDTH), F32), pltpu.VMEM((8, WIDTH), F32),
+            pltpu.VMEM((8, WIDTH), F32), pltpu.VMEM((8, WIDTH), F32), pltpu.VMEM((8, HIDDEN), F32),
             pltpu.VMEM((SLOTS, FRAMES, WIDTH), BF16),
-            pltpu.VMEM((WIDTH, WIDTH), BF16), pltpu.VMEM((WIDTH, WIDTH), BF16), pltpu.VMEM((WIDTH, WIDTH), BF16),
-            pltpu.VMEM((WIDTH, WIDTH), BF16),
-            pltpu.VMEM((HIDDEN, WIDTH), BF16), pltpu.VMEM((HIDDEN, WIDTH), BF16),
+            pltpu.VMEM((2 * WIDTH, WIDTH), BF16), pltpu.VMEM((WIDTH, WIDTH), BF16), pltpu.VMEM((WIDTH, WIDTH), BF16),
+            pltpu.VMEM((WIDTH, HIDDEN), BF16), pltpu.VMEM((HIDDEN, WIDTH), BF16),
             pltpu.VMEM((4, 8, WIDTH), F32),
-            pltpu.VMEM((FRAMES, WIDTH), BF16), pltpu.VMEM((FRAMES, WIDTH), BF16), pltpu.VMEM((WIDTH, FRAMES), BF16),
-            pltpu.VMEM((FRAMES, WIDTH), BF16), pltpu.VMEM((FRAMES, WIDTH), BF16),
+            pltpu.VMEM((FRAMES, WIDTH), BF16), pltpu.VMEM((FRAMES, 2 * WIDTH), BF16), pltpu.VMEM((WIDTH, FRAMES), BF16),
+            pltpu.VMEM((FRAMES, WIDTH), BF16),
             pltpu.VMEM((SLOTS, FRAMES, WIDTH), BF16),
             pltpu.VMEM((FRAMES, 2 * WIDTH), BF16),
             pltpu.VMEM((SLOTS, FRAMES, WIDTH), F32),
-            pltpu.VMEM((8, WIDTH), F32),
+            pltpu.VMEM((8, 2 * WIDTH), F32),
             dma((SLOTS, 3)), dma((SLOTS, 3)), dma((SLOTS,)),
             dma((8, 5)), dma((8, 5)), dma((8,)),
             dma((3,)), dma((3,)),
@@ -405,28 +410,32 @@
     )(x, *weights, *vectors)
 
 
-def cache_kernel(tp_ref, e_ref, wk_ref, wv_ref, bias_ref, k_ref, v_ref, enc_ref, shift):
+def cache_kernel(tp_ref, e_ref, wk_hbm, wv_hbm, bias_ref, k_ref, v_ref, enc_ref, weights, shift, sems):
     @pl.when(pl.program_id(0) == 0)
     def _():
-        rows = jnp.concatenate([bias_ref[...].astype(F32), jnp.zeros((4, 192), F32)], axis=0)
+        copies = [pltpu.make_async_copy(src.at[layer], weights.at[pl.ds(which * WIDTH + layer * LOC_COLS, LOC_COLS), :], sems.at[which, layer])
+                  for which, src in enumerate((wk_hbm, wv_hbm)) for layer in range(4)]
+        for copy in copies:
+            copy.start()
+        rows = jnp.concatenate([bias_ref[...].astype(F32), jnp.zeros((4, LOC_COLS), F32)], axis=0)
         for layer in range(4):
             pick = (lax.broadcasted_iota(jnp.int32, (8, 128), 0) == layer).astype(F32)
-            shift[layer * 192:layer * 192 + 192, :] = dot(rows, pick, TN)
+            shift[layer * LOC_COLS:(layer + 1) * LOC_COLS, :] = dot(rows, pick, TN)
+        for copy in copies:
+            copy.wait()
 
     enc_ref[0] = e_ref[0, pl.ds(pl.multiple_of(tp_ref[0] * LOC_FRAMES, LOC_FRAMES), LOC_FRAMES), :]
-    for first in range(0, FRAMES, 256):
-        frames = slice(first, first + 256)
-        keys = dot(wk_ref[...].reshape(WIDTH, WIDTH), e_ref[0, frames, :], NT).astype(BF16)
-        values = (dot(wv_ref[...].reshape(WIDTH, WIDTH), e_ref[0, frames, :], NT) + jnp.concatenate([shift[...]] * 2, axis=1)).astype(BF16)
-        for layer in range(4):
-            k_ref[layer, 0, :, frames] = keys[layer * 192:layer * 192 + 192, :]
-            v_ref[layer, 0, :, frames] = values[layer * 192:layer * 192 + 192, :]
+    both = dot(weights[...], e_ref[0], NT)
+    for layer in range(4):
+        rows = slice(layer * LOC_COLS, (layer + 1) * LOC_COLS)
+        k_ref[layer, 0] = both[rows, :].astype(BF16)
+        v_ref[layer, 0] = (both[WIDTH + layer * LOC_COLS:WIDTH + (layer + 1) * LOC_COLS, :] + jnp.concatenate([shift[rows, :]] * 4, axis=1)).astype(BF16)
 
 
 def caches(tp, e_all, wck_t, wcv_t, bias):
-    cache = jax.ShapeDtypeStruct((4, CLIPS, 192, FRAMES), BF16)
-    cache_spec = pl.BlockSpec((4, 1, 192, FRAMES), lambda clip, tp_ref: (0, clip, 0, 0))
-    whole = lambda clip, tp_ref: (0, 0, 0)
+    cache = jax.ShapeDtypeStruct((4, CLIPS, LOC_COLS, FRAMES), BF16)
+    cache_spec = pl.BlockSpec((4, 1, LOC_COLS, FRAMES), lambda clip, tp_ref: (0, clip, 0, 0))
+    any_spec = pl.BlockSpec(memory_space=pl.ANY)
     return pl.pallas_call(
         cache_kernel,
         out_shape=(cache, cache, jax.ShapeDtypeStruct((CLIPS, LOC_FRAMES, WIDTH), BF16)),
@@ -435,11 +444,11 @@
             grid=(CLIPS,),
             in_specs=[
                 pl.BlockSpec((1, FRAMES, WIDTH), lambda clip, tp_ref: (clip, 0, 0)),
-                pl.BlockSpec((4, 192, WIDTH), whole), pl.BlockSpec((4, 192, WIDTH), whole),
-                pl.BlockSpec((4, 192), lambda clip, tp_ref: (0, 0)),
+                any_spec, any_spec,
+                pl.BlockSpec((4, LOC_COLS), lambda clip, tp_ref: (0, 0)),
             ],
             out_specs=(cache_spec, cache_spec, pl.BlockSpec((1, LOC_FRAMES, WIDTH), lambda clip, tp_ref: (clip, 0, 0))),
-            scratch_shapes=[pltpu.VMEM((WIDTH, 128), F32)],
+            scratch_shapes=[pltpu.VMEM((2 * WIDTH, WIDTH), BF16), pltpu.VMEM((WIDTH, 128), F32), pltpu.SemaphoreType.DMA((2, 4))],
         ),
         compiler_params=pltpu.CompilerParams(dimension_semantics=("arbitrary",), vmem_limit_bytes=64 * 1024 * 1024 - 128 * 1024),
         name="caches",

time: 195 us -> 185 us (0.949)
  Pallas kernels: 194 us -> 183 us
    pallas_call x1, Pallas kernels: 165 us -> 154 us  [encode(): pl.pallas_call(encoder_kernel, out_shape=jax.ShapeDtypeStruct((CLIPS, FRA...]
where the time goes in v3:
time: 185 us; the launch traced here: 184 us
  Pallas kernels  183 us (99%)
    pallas_call x1, Pallas kernels, encode(): pl.pallas_call(encoder_kernel, out_shape=jax.ShapeDtypeStruct((CLIPS, FRA...  154 us
    pallas_call x1, Pallas kernels, caches(): pl.pallas_call(cache_kernel, out_shape=(cache, cache, jax.ShapeDtypeStruc...  29.5 us

profile of v3, /device:TPU:0, one launch (start us, length us, event | category | flops | bytes accessed | tf_op | source)
XLA Modules:
  0.0 184.1 jit_solution(16640100266544257400)
XLA Ops:
  0.6 154.0 %encoder.1.e_ref = bf16[16,512,768]{2,1,0:T(8,128)(2,1)} custom-call(bf16[16,128,768]{2,1,0:T(8,128)(2,1)} %x_hbm.1, bf16[192,768]{1,0:T(8,128)(2,1)} %bitcast.14, bf16[192,768]{1,0:T(8,128)(2,1)} %bitcast.15, bf16[192,768]{1,0:T(8,128)(2,1)} %bitcast.16, bf16[192,768]{1,0:T(8,128)(2,1)} %wo_hbm.1, bf16[768,768]{1,0:T(8,128)(2,1)} %w1_hbm.1, ...), custom_call_target="tpu_custom_call" | custom-call | tf_op jit(solution)/shard_map/encoder/pallas_call | solution.py:386
  154.7 29.5 %caches.1 = (bf16[4,16,192,512]{3,2,1,0:T(8,128)(2,1)}, bf16[4,16,192,512]{3,2,1,0:T(8,128)(2,1)}, bf16[16,128,768]{2,1,0:T(8,128)(2,1)}) custom-call(s32[1]{0:T(128)} %bitcast.tp_ref, bf16[16,512,768]{2,1,0:T(8,128)(2,1)} %encoder.1.e_ref, bf16[4,192,768]{2,1,0:T(8,128)(2,1)} %bitcast.12, bf16[4,192,768]{2,1,0:T(8,128)(2,1)} %bitcast.13, ...), custom_call_target="tpu_custom_call" | custom-call | tf_op jit(solution)/shard_map/caches/pallas_call | solution.py:439

commit v4 on v3

--- a/solution.py
+++ b/solution.py
@@ -17,16 +17,17 @@
 CLIPS, FRAMES, WIDTH, HIDDEN = 16, 512, 768, 3072
 LOC_FRAMES, LOC_COLS = FRAMES // 4, WIDTH // 4
 WIDE = (slice(0, 512), slice(512, 768))
-SHARED, ONLY = 4, 2
+SHARED, ONLY = 6, 1
 SLOTS = SHARED + ONLY
 LAG = 3
 LN_ROWS = 64
-SEND_ORDER = ("q", "k", "v", 0, "o", 1, 2, "w1a", "w1b", 3, "w2a", "w2b", 4, 5)
+SEND_ORDER = ("q", "k", "v", 0, "o", 1, 2, "w1a", "w1b", 3, "w2a", "w2b", 4, 5, 6)
 RELAYS = {
     (3, 0): ((1, "w1a"), (1, "w1b")),
     (3, 1): ((2, "w1a"), (2, "w1b"), (1, "w2a"), (1, "w2b")),
     (3, 2): ((2, "w2a"), (2, "w2b")),
 }
+OUT_SLOTS = 6
 
 NT = (((1,), (1,)), ((), ()))
 NN = (((1,), (0,)), ((), ()))
@@ -410,57 +411,93 @@
     )(x, *weights, *vectors)
 
 
-def cache_kernel(tp_ref, e_ref, wk_hbm, wv_hbm, bias_ref, k_ref, v_ref, enc_ref, weights, shift, sems):
-    @pl.when(pl.program_id(0) == 0)
-    def _():
-        copies = [pltpu.make_async_copy(src.at[layer], weights.at[pl.ds(which * WIDTH + layer * LOC_COLS, LOC_COLS), :], sems.at[which, layer])
-                  for which, src in enumerate((wk_hbm, wv_hbm)) for layer in range(4)]
-        for copy in copies:
-            copy.start()
-        rows = jnp.concatenate([bias_ref[...].astype(F32), jnp.zeros((4, LOC_COLS), F32)], axis=0)
-        for layer in range(4):
-            pick = (lax.broadcasted_iota(jnp.int32, (8, 128), 0) == layer).astype(F32)
-            shift[layer * LOC_COLS:(layer + 1) * LOC_COLS, :] = dot(rows, pick, TN)
-        for copy in copies:
+def cache_kernel(e_hbm, wk_hbm, wv_hbm, bias_ref, k_hbm, v_hbm, enc_hbm, weights, shift, ebuf, obuf, w_sem, e_sem, out_sem, enc_sem):
+    tp = lax.axis_index("tp")
+
+    def load(clip):
+        return pltpu.make_async_copy(e_hbm.at[clip], ebuf.at[clip], e_sem.at[clip])
+
+    def stores(clip, slot):
+        copies = []
+        for which, dst in enumerate((k_hbm, v_hbm)):
+            for layer in range(4):
+                rows = pl.ds(which * WIDTH + layer * LOC_COLS, LOC_COLS)
+                copies.append(pltpu.make_async_copy(obuf.at[slot, rows, :], dst.at[layer, clip], out_sem.at[slot, which * 4 + layer]))
+        return copies
+
+    def enc_store(clip):
+        own = pl.ds(pl.multiple_of(tp * LOC_FRAMES, LOC_FRAMES), LOC_FRAMES)
+        return pltpu.make_async_copy(ebuf.at[clip, own, :], enc_hbm.at[clip], enc_sem.at[clip])
+
+    load(0).start()
+    weight_loads = [pltpu.make_async_copy(src.at[layer], weights.at[pl.ds(which * WIDTH + layer * LOC_COLS, LOC_COLS), :], w_sem.at[which, layer])
+                    for which, src in enumerate((wk_hbm, wv_hbm)) for layer in range(4)]
+    for copy in weight_loads:
+        copy.start()
+    for clip in range(1, CLIPS):
+        load(clip).start()
+    rows = jnp.concatenate([bias_ref[...].astype(F32), jnp.zeros((4, LOC_COLS), F32)], axis=0)
+    for layer in range(4):
+        pick = (lax.broadcasted_iota(jnp.int32, (8, 128), 0) == layer).astype(F32)
+        shift[layer * LOC_COLS:(layer + 1) * LOC_COLS, :] = dot(rows, pick, TN)
+    for copy in weight_loads:
+        copy.wait()
+
+    def body(step, _):
+        for half in range(2):
+            clip = 2 * step + half
+            slot = clip % OUT_SLOTS
+            load(clip).wait()
+            enc_store(clip).start()
+
+            @pl.when(clip >= OUT_SLOTS)
+            def _():
+                for copy in stores(clip - OUT_SLOTS, slot):
+                    copy.wait()
+
+        for half in range(2):
+            clip = 2 * step + half
+            slot = clip % OUT_SLOTS
+            obuf[slot, 0:WIDTH, :] = dot(weights[0:WIDTH, :], ebuf[clip], NT).astype(BF16)
+            obuf[slot, WIDTH:2 * WIDTH, :] = (dot(weights[WIDTH:2 * WIDTH, :], ebuf[clip], NT) + jnp.concatenate([shift[...]] * 4, axis=1)).astype(BF16)
+        for half in range(2):
+            clip = 2 * step + half
+            for copy in stores(clip, clip % OUT_SLOTS):
+                copy.start()
+        return 0
+
+    lax.fori_loop(0, CLIPS // 2, body, 0)
+    for clip in range(CLIPS - OUT_SLOTS, CLIPS):
+        for copy in stores(clip, clip % OUT_SLOTS):
             copy.wait()
-
-    enc_ref[0] = e_ref[0, pl.ds(pl.multiple_of(tp_ref[0] * LOC_FRAMES, LOC_FRAMES), LOC_FRAMES), :]
-    both = dot(weights[...], e_ref[0], NT)
-    for layer in range(4):
-        rows = slice(layer * LOC_COLS, (layer + 1) * LOC_COLS)
-        k_ref[layer, 0] = both[rows, :].astype(BF16)
-        v_ref[layer, 0] = (both[WIDTH + layer * LOC_COLS:WIDTH + (layer + 1) * LOC_COLS, :] + jnp.concatenate([shift[rows, :]] * 4, axis=1)).astype(BF16)
-
-
-def caches(tp, e_all, wck_t, wcv_t, bias):
+    for clip in range(CLIPS):
+        enc_store(clip).wait()
+
+
+def caches(e_all, wck_t, wcv_t, bias):
     cache = jax.ShapeDtypeStruct((4, CLIPS, LOC_COLS, FRAMES), BF16)
-    cache_spec = pl.BlockSpec((4, 1, LOC_COLS, FRAMES), lambda clip, tp_ref: (0, clip, 0, 0))
     any_spec = pl.BlockSpec(memory_space=pl.ANY)
+    dma = pltpu.SemaphoreType.DMA
     return pl.pallas_call(
         cache_kernel,
         out_shape=(cache, cache, jax.ShapeDtypeStruct((CLIPS, LOC_FRAMES, WIDTH), BF16)),
-        grid_spec=pltpu.PrefetchScalarGridSpec(
-            num_scalar_prefetch=1,
-            grid=(CLIPS,),
-            in_specs=[
-                pl.BlockSpec((1, FRAMES, WIDTH), lambda clip, tp_ref: (clip, 0, 0)),
-                any_spec, any_spec,
-                pl.BlockSpec((4, LOC_COLS), lambda clip, tp_ref: (0, 0)),
-            ],
-            out_specs=(cache_spec, cache_spec, pl.BlockSpec((1, LOC_FRAMES, WIDTH), lambda clip, tp_ref: (clip, 0, 0))),
-            scratch_shapes=[pltpu.VMEM((2 * WIDTH, WIDTH), BF16), pltpu.VMEM((WIDTH, 128), F32), pltpu.SemaphoreType.DMA((2, 4))],
-        ),
-        compiler_params=pltpu.CompilerParams(dimension_semantics=("arbitrary",), vmem_limit_bytes=64 * 1024 * 1024 - 128 * 1024),
+        in_specs=[any_spec, any_spec, any_spec, pl.BlockSpec(memory_space=pltpu.VMEM)],
+        out_specs=(any_spec, any_spec, any_spec),
+        scratch_shapes=[
+            pltpu.VMEM((2 * WIDTH, WIDTH), BF16), pltpu.VMEM((WIDTH, 128), F32),
+            pltpu.VMEM((CLIPS, FRAMES, WIDTH), BF16), pltpu.VMEM((OUT_SLOTS, 2 * WIDTH, FRAMES), BF16),
+            dma((2, 4)), dma((CLIPS,)), dma((OUT_SLOTS, 8)), dma((CLIPS,)),
+        ],
+        compiler_params=pltpu.CompilerParams(vmem_limit_bytes=64 * 1024 * 1024 - 128 * 1024),
         name="caches",
-    )(tp, e_all, wck_t, wcv_t, bias)
+    )(e_all, wck_t, wcv_t, bias)
 
 
 def device_body(hidden_loc, ln1_gain, ln1_bias, w_q, b_q, w_k, w_v, b_v, w_o, b_o, ln2_gain, ln2_bias, w_fc1, b_fc1, w_fc2, b_fc2, post_gain, post_bias, w_ck, w_cv, b_cv):
     weights = (w_q.T, w_k.T, w_v.T, w_o, w_fc1, w_fc2)
     vectors = (ln1_gain, ln1_bias, ln2_gain, ln2_bias, post_gain, post_bias, b_o, b_fc2, b_fc1, b_q, b_v)
     e_all = encode(hidden_loc, weights, vectors)
-    tp = lax.axis_index("tp").astype(jnp.int32).reshape(1)
-    k_t, v_t, enc_loc = caches(tp, e_all, w_ck.transpose(0, 2, 1), w_cv.transpose(0, 2, 1), b_cv)
+    k_t, v_t, enc_loc = caches(e_all, w_ck.transpose(0, 2, 1), w_cv.transpose(0, 2, 1), b_cv)
     shape = (4, CLIPS, FRAMES, 3, HEAD_DIM)
     return enc_loc, k_t.transpose(0, 1, 3, 2).reshape(shape), v_t.transpose(0, 1, 3, 2).reshape(shape)
 

time: 185 us -> 199 us (1.076)
  Pallas kernels: 183 us -> 198 us
    pallas_call x1, Pallas kernels: 154 us -> 168 us  [encode(): pl.pallas_call(encoder_kernel, out_shape=jax.ShapeDtypeStruct((CLIPS, FRA...]
where the time goes in v4:
time: 199 us
  Pallas kernels  198 us (99%)
    pallas_call x1, Pallas kernels, encode(): pl.pallas_call(encoder_kernel, out_shape=jax.ShapeDtypeStruct((CLIPS, FRA...  168 us
    pallas_call x1, Pallas kernels, caches(): pl.pallas_call(cache_kernel, out_shape=(cache, cache, jax.ShapeDtypeStruc...  29.7 us

profile of v4, /device:TPU:0, one launch (start us, length us, event | category | flops | bytes accessed | tf_op | source)
XLA Modules:
  0.0 198.9 jit_solution(6407501165528212923)
XLA Ops:
  0.6 168.5 %encoder.1.e_hbm = bf16[16,512,768]{2,1,0:T(8,128)(2,1)} custom-call(bf16[16,128,768]{2,1,0:T(8,128)(2,1)} %x_hbm.1, bf16[192,768]{1,0:T(8,128)(2,1)} %bitcast.13, bf16[192,768]{1,0:T(8,128)(2,1)} %bitcast.14, bf16[192,768]{1,0:T(8,128)(2,1)} %bitcast.15, bf16[192,768]{1,0:T(8,128)(2,1)} %wo_hbm.1, bf16[768,768]{1,0:T(8,128)(2,1)} %w1_hbm.1, ...), custom_call_target="tpu_custom_call" | custom-call | tf_op jit(solution)/shard_map/encoder/pallas_call | solution.py:387
  169.1 29.7 %caches.1 = (bf16[4,16,192,512]{3,2,1,0:T(8,128)(2,1)}, bf16[4,16,192,512]{3,2,1,0:T(8,128)(2,1)}, bf16[16,128,768]{2,1,0:T(8,128)(2,1)}) custom-call(bf16[16,512,768]{2,1,0:T(8,128)(2,1)} %encoder.1.e_hbm, bf16[4,192,768]{2,1,0:T(8,128)(2,1)} %bitcast.11, bf16[4,192,768]{2,1,0:T(8,128)(2,1)} %bitcast.12, bf16[4,192]{1,0:T(4,128)(2,1)} %bias_ref.1), custom_call_target="tpu_custom_call" | custom-call | tf_op jit(solution)/shard_map/caches/pallas_call | solution.py:481

commit v5 on v4

--- a/solution.py
+++ b/solution.py
@@ -17,17 +17,17 @@
 CLIPS, FRAMES, WIDTH, HIDDEN = 16, 512, 768, 3072
 LOC_FRAMES, LOC_COLS = FRAMES // 4, WIDTH // 4
 WIDE = (slice(0, 512), slice(512, 768))
-SHARED, ONLY = 6, 1
+SHARED, ONLY = 4, 2
 SLOTS = SHARED + ONLY
-LAG = 3
+LAG = SLOTS // 2
 LN_ROWS = 64
-SEND_ORDER = ("q", "k", "v", 0, "o", 1, 2, "w1a", "w1b", 3, "w2a", "w2b", 4, 5, 6)
+SEND_ORDER = ("q", "k", "v", 0, "o", 1, 2, "w1a", "w1b", 3, "w2a", "w2b", 4, 5)
 RELAYS = {
-    (3, 0): ((1, "w1a"), (1, "w1b")),
-    (3, 1): ((2, "w1a"), (2, "w1b"), (1, "w2a"), (1, "w2b")),
-    (3, 2): ((2, "w2a"), (2, "w2b")),
+    (0, 1): ((1, "o"),), (0, 5): ((2, "o"),),
+    (2, 2): ((1, "w1a"),), (2, 5): ((1, "w1b"), (2, "w1a")),
+    (3, 0): ((2, "w1b"),), (3, 3): ((1, "w2a"),), (3, 5): ((1, "w2b"), (2, "w2a")),
 }
-OUT_SLOTS = 6
+OUT_SLOTS, AHEAD = 6, 4
 
 NT = (((1,), (1,)), ((), ()))
 NN = (((1,), (0,)), ((), ()))
@@ -170,6 +170,10 @@
         sem = SLOTS + ONLY + slot
         return remote(e_hbm.at[clip], e_hbm.at[clip], e_send.at[sem], e_recv.at[sem], sib)
 
+    barrier = pltpu.get_barrier_semaphore()
+    for device in (sib, far, diag, side):
+        pl.semaphore_signal(barrier, inc=1, device_id=device, device_id_type=MESH)
+
     for row, ref in enumerate((g1_ref, s1_ref, g2_ref, s2_ref, g3_ref, s3_ref, bo_ref, b2_ref)):
         rep_ref[row:row + 1, :] = ref[...].astype(F32).reshape(1, WIDTH)
     place = lax.broadcasted_iota(jnp.int32, (192, WIDTH), 0) + tp * 192 == lax.broadcasted_iota(jnp.int32, (192, WIDTH), 1)
@@ -181,15 +185,11 @@
     loc[3:8, :] = jnp.zeros((5, WIDTH), F32)
     small[tp] = loc[...]
 
-    barrier = pltpu.get_barrier_semaphore()
-    for device in (sib, far, diag, side):
-        pl.semaphore_signal(barrier, inc=1, device_id=device, device_id_type=MESH)
     pl.semaphore_wait(barrier, 4)
 
+    for link in (1, 2, 0):
+        s_copy(link, tp).start()
     for item in SEND_ORDER:
-        if item == 0:
-            for link in range(3):
-                s_copy(link, tp).start()
         if isinstance(item, str):
             w_start(item)
         else:
@@ -198,16 +198,18 @@
             x_local(item).start()
             x_copy(item, 0).start()
 
+    w_stage1("q")
+    w_stage1("k")
+    w_stage2("q")
+    w_stage1("v")
+    w_stage2("k")
     for link, owner in enumerate((t_sib, t_far, t_diag)):
         s_copy(link, owner).wait_recv()
     bias[0:1, 0:WIDTH] = small[0, 1:2, :] + small[1, 1:2, :] + small[2, 1:2, :] + small[3, 1:2, :]
     bias[0:1, WIDTH:2 * WIDTH] = small[0, 2:3, :] + small[1, 2:3, :] + small[2, 2:3, :] + small[3, 2:3, :]
     for owner in range(4):
         b1_row[0:1, owner * WIDTH:owner * WIDTH + WIDTH] = small[owner, 0:1, :]
-    for name in ("q", "k", "v"):
-        w_stage1(name)
-    for name in ("q", "k", "v"):
-        w_stage2(name)
+    w_stage2("v")
     for name in ("q", "k", "v"):
         w_wait_near(name)
         w_wait_far(name)
@@ -236,6 +238,12 @@
         keep = [(lane < 64).astype(F32).astype(BF16), (lane >= 64).astype(F32).astype(BF16)]
 
         def pair_body(pair, _):
+            for (when, where), todo in RELAYS.items():
+                @pl.when((step == when) & (pair == where))
+                def _():
+                    for stage, name in todo:
+                        (w_stage1 if stage == 1 else w_stage2)(name)
+
             cols = pl.ds(pl.multiple_of(pair * 128, 128), 128)
             keys_t = ktbuf[cols, :]
             values = qvbuf[:, pl.ds(pl.multiple_of(WIDTH + pair * 128, 128), 128)]
@@ -259,8 +267,6 @@
 
         @pl.when(step == 0)
         def _():
-            w_stage1("o")
-            w_stage2("o")
             w_wait_near("o")
             w_wait_far("o")
 
@@ -318,46 +324,33 @@
 
     mlp_units = ("w1a", "w1b", "w2a", "w2b")
 
-    def relays(step, place):
-        for (when, where), todo in RELAYS.items():
-            if where == place:
-                @pl.when(step == when)
-                def _():
-                    for stage, name in todo:
-                        (w_stage1 if stage == 1 else w_stage2)(name)
-
     def step_body(step, _):
-        relays(step, 0)
-
-        @pl.when(step < SLOTS)
-        def _():
-            attention(step, step)
-
-        relays(step, 1)
+        attention(step, step)
 
         @pl.when(step == 0)
         def _():
             for name in mlp_units:
                 w_wait_near(name)
 
-        @pl.when(step < SLOTS)
-        def _():
-            mlp_near(step)
-
-        relays(step, 2)
+        mlp_near(step)
 
         @pl.when(step == LAG)
         def _():
+            w_stage2("w2b")
             for name in mlp_units:
                 w_wait_far(name)
 
         @pl.when(step >= LAG)
         def _():
-            mlp_far(step - LAG)
+            def far_body(turn, _):
+                mlp_far(2 * (step - LAG) + turn)
+                return 0
+
+            lax.fori_loop(0, 2, far_body, 0)
 
         return 0
 
-    lax.fori_loop(0, SLOTS + LAG, step_body, 0)
+    lax.fori_loop(0, SLOTS, step_body, 0)
 
     for slot in range(ONLY):
         clip = only_clip(other_chip, core, slot)
@@ -434,7 +427,7 @@
                     for which, src in enumerate((wk_hbm, wv_hbm)) for layer in range(4)]
     for copy in weight_loads:
         copy.start()
-    for clip in range(1, CLIPS):
+    for clip in range(1, AHEAD):
         load(clip).start()
     rows = jnp.concatenate([bias_ref[...].astype(F32), jnp.zeros((4, LOC_COLS), F32)], axis=0)
     for layer in range(4):
@@ -449,6 +442,10 @@
             slot = clip % OUT_SLOTS
             load(clip).wait()
             enc_store(clip).start()
+
+            @pl.when(clip + AHEAD < CLIPS)
+            def _():
+                load(clip + AHEAD).start()
 
             @pl.when(clip >= OUT_SLOTS)
             def _():

time: 199 us -> 172 us (0.86)
  Pallas kernels: 198 us -> 171 us
    pallas_call x1, Pallas kernels: 168 us -> 144 us  [encode(): pl.pallas_call(encoder_kernel, out_shape=jax.ShapeDtypeStruct((CLIPS, FRA...]
    pallas_call x1, Pallas kernels: 29.7 us -> 27 us  [caches(): pl.pallas_call(cache_kernel, out_shape=(cache, cache, jax.ShapeDtypeStruc...]
where the time goes in v5:
time: 172 us
  Pallas kernels  171 us (99%)
    pallas_call x1, Pallas kernels, encode(): pl.pallas_call(encoder_kernel, out_shape=jax.ShapeDtypeStruct((CLIPS, FRA...  144 us
    pallas_call x1, Pallas kernels, caches(): pl.pallas_call(cache_kernel, out_shape=(cache, cache, jax.ShapeDtypeStruc...  27 us

profile of v5, /device:TPU:0, one launch (start us, length us, event | category | flops | bytes accessed | tf_op | source)
XLA Modules:
  0.0 171.7 jit_solution(6394622771590359631)
XLA Ops:
  0.6 144.0 %encoder.1.e_hbm = bf16[16,512,768]{2,1,0:T(8,128)(2,1)} custom-call(bf16[16,128,768]{2,1,0:T(8,128)(2,1)} %x_hbm.1, bf16[192,768]{1,0:T(8,128)(2,1)} %bitcast.13, bf16[192,768]{1,0:T(8,128)(2,1)} %bitcast.14, bf16[192,768]{1,0:T(8,128)(2,1)} %bitcast.15, bf16[192,768]{1,0:T(8,128)(2,1)} %wo_hbm.1, bf16[768,768]{1,0:T(8,128)(2,1)} %w1_hbm.1, ...), custom_call_target="tpu_custom_call" | custom-call | tf_op jit(solution)/shard_map/encoder/pallas_call | solution.py:380
  144.7 27.0 %caches.1 = (bf16[4,16,192,512]{3,2,1,0:T(8,128)(2,1)}, bf16[4,16,192,512]{3,2,1,0:T(8,128)(2,1)}, bf16[16,128,768]{2,1,0:T(8,128)(2,1)}) custom-call(bf16[16,512,768]{2,1,0:T(8,128)(2,1)} %encoder.1.e_hbm, bf16[4,192,768]{2,1,0:T(8,128)(2,1)} %bitcast.11, bf16[4,192,768]{2,1,0:T(8,128)(2,1)} %bitcast.12, bf16[4,192]{1,0:T(4,128)(2,1)} %bias_ref.1), custom_call_target="tpu_custom_call" | custom-call | tf_op jit(solution)/shard_map/caches/pallas_call | solution.py:478

commit v6 on v5

--- a/solution.py
+++ b/solution.py
@@ -19,13 +19,15 @@
 WIDE = (slice(0, 512), slice(512, 768))
 SHARED, ONLY = 4, 2
 SLOTS = SHARED + ONLY
-LAG = SLOTS // 2
+LAG = 4
+FAR_TURNS = 3
 LN_ROWS = 64
 SEND_ORDER = ("q", "k", "v", 0, "o", 1, 2, "w1a", "w1b", 3, "w2a", "w2b", 4, 5)
 RELAYS = {
-    (0, 1): ((1, "o"),), (0, 5): ((2, "o"),),
-    (2, 2): ((1, "w1a"),), (2, 5): ((1, "w1b"), (2, "w1a")),
-    (3, 0): ((2, "w1b"),), (3, 3): ((1, "w2a"),), (3, 5): ((1, "w2b"), (2, "w2a")),
+    (0, 2): ((1, "o"),), (0, 5): ((2, "o"),),
+    (2, 0): ((1, "w1a"),), (2, 5): ((1, "w1b"),),
+    (3, 1): ((2, "w1a"),), (3, 3): ((2, "w1b"),), (3, 5): ((1, "w2a"),),
+    (4, 0): ((1, "w2b"),), (4, 3): ((2, "w2a"),),
 }
 OUT_SLOTS, AHEAD = 6, 4
 
@@ -343,10 +345,10 @@
         @pl.when(step >= LAG)
         def _():
             def far_body(turn, _):
-                mlp_far(2 * (step - LAG) + turn)
+                mlp_far(FAR_TURNS * (step - LAG) + turn)
                 return 0
 
-            lax.fori_loop(0, 2, far_body, 0)
+            lax.fori_loop(0, FAR_TURNS, far_body, 0)
 
         return 0
 

time: 172 us -> 171 us (level)
  no operation moved by 1% of the time
where the time goes in v6:
time: 171 us
  Pallas kernels  171 us (100%)
    pallas_call x1, Pallas kernels, encode(): pl.pallas_call(encoder_kernel, out_shape=jax.ShapeDtypeStruct((CLIPS, FRA...  143 us
    pallas_call x1, Pallas kernels, caches(): pl.pallas_call(cache_kernel, out_shape=(cache, cache, jax.ShapeDtypeStruc...  27 us

profile of v6, /device:TPU:0, one launch (start us, length us, event | category | flops | bytes accessed | tf_op | source)
XLA Modules:
  0.0 171.2 jit_solution(347820534905287351)
XLA Ops:
  0.6 143.5 %encoder.1.e_hbm = bf16[16,512,768]{2,1,0:T(8,128)(2,1)} custom-call(bf16[16,128,768]{2,1,0:T(8,128)(2,1)} %x_hbm.1, bf16[192,768]{1,0:T(8,128)(2,1)} %bitcast.13, bf16[192,768]{1,0:T(8,128)(2,1)} %bitcast.14, bf16[192,768]{1,0:T(8,128)(2,1)} %bitcast.15, bf16[192,768]{1,0:T(8,128)(2,1)} %wo_hbm.1, bf16[768,768]{1,0:T(8,128)(2,1)} %w1_hbm.1, ...), custom_call_target="tpu_custom_call" | custom-call | tf_op jit(solution)/shard_map/encoder/pallas_call | solution.py:382
  144.1 27.0 %caches.1 = (bf16[4,16,192,512]{3,2,1,0:T(8,128)(2,1)}, bf16[4,16,192,512]{3,2,1,0:T(8,128)(2,1)}, bf16[16,128,768]{2,1,0:T(8,128)(2,1)}) custom-call(bf16[16,512,768]{2,1,0:T(8,128)(2,1)} %encoder.1.e_hbm, bf16[4,192,768]{2,1,0:T(8,128)(2,1)} %bitcast.11, bf16[4,192,768]{2,1,0:T(8,128)(2,1)} %bitcast.12, bf16[4,192]{1,0:T(4,128)(2,1)} %bias_ref.1), custom_call_target="tpu_custom_call" | custom-call | tf_op jit(solution)/shard_map/caches/pallas_call | solution.py:480

commit v7 on v6

--- a/solution.py
+++ b/solution.py
@@ -19,6 +19,7 @@
 WIDE = (slice(0, 512), slice(512, 768))
 SHARED, ONLY = 4, 2
 SLOTS = SHARED + ONLY
+OTHERS = CLIPS - SLOTS
 LAG = 4
 FAR_TURNS = 3
 LN_ROWS = 64
@@ -59,10 +60,27 @@
     return ref.at[pl.ds(pl.multiple_of(start, 16), count), :]
 
 
+def cache_weight_loads(wk_hbm, wv_hbm, dst, sems):
+    return [pltpu.make_async_copy(src.at[layer], dst.at[pl.ds(which * WIDTH + layer * LOC_COLS, LOC_COLS), :], sems.at[which, layer])
+            for which, src in enumerate((wk_hbm, wv_hbm)) for layer in range(4)]
+
+
+def lay_out_shift(bias_ref, shift):
+    rows = jnp.concatenate([bias_ref[...].astype(F32), jnp.zeros((4, LOC_COLS), F32)], axis=0)
+    for layer in range(4):
+        pick = (lax.broadcasted_iota(jnp.int32, (8, 128), 0) == layer).astype(F32)
+        shift[layer * LOC_COLS:(layer + 1) * LOC_COLS, :] = dot(rows, pick, TN)
+
+
+def cache_products(dst, slot, weights, shift, clips, clip):
+    dst[slot, 0:WIDTH, :] = dot(weights[0:WIDTH, :], clips[clip], NT).astype(BF16)
+    dst[slot, WIDTH:2 * WIDTH, :] = (dot(weights[WIDTH:2 * WIDTH, :], clips[clip], NT) + jnp.concatenate([shift[...]] * 4, axis=1)).astype(BF16)
+
+
 def encoder_kernel(x_hbm, wq_hbm, wk_hbm, wv_hbm, wo_hbm, w1_hbm, w2_hbm,
-                   g1_ref, s1_ref, g2_ref, s2_ref, g3_ref, s3_ref, bo_ref, b2_ref, b1_ref, bq_ref, bv_ref, e_hbm,
-                   rep_ref, loc, b1_row, xbuf, wqv, wk, wo, w1, w2, small, abuf, qvbuf, ktbuf, obuf, mbuf, gbuf, acc, bias,
-                   x_send, x_recv, x_loc, w_send, w_recv, w_loc, s_send, s_recv, e_send, e_recv, e_loc):
+                   g1_ref, s1_ref, g2_ref, s2_ref, g3_ref, s3_ref, bo_ref, b2_ref, b1_ref, bq_ref, bv_ref, wck_hbm, wcv_hbm, bcv_ref, e_hbm, part_hbm,
+                   rep_ref, loc, b1_row, xbuf, wqv, wk, wo, w1, w2, small, abuf, qvbuf, ktbuf, obuf, mbuf, gbuf, acc, bias, cw, shift, cbuf,
+                   x_send, x_recv, x_loc, w_send, w_recv, w_loc, s_send, s_recv, e_send, e_recv, e_loc, cw_sem, c_sem):
     group, tp = lax.axis_index("dp"), lax.axis_index("tp")
     chip, core = tp // 2, tp % 2
     other_chip, other_core = 1 - chip, 1 - core
@@ -199,6 +217,11 @@
             x_copy(item, 2).start()
             x_local(item).start()
             x_copy(item, 0).start()
+
+    cache_loads = cache_weight_loads(wck_hbm, wcv_hbm, cw, cw_sem)
+    for copy in cache_loads:
+        copy.start()
+    lay_out_shift(bcv_ref, shift)
 
     w_stage1("q")
     w_stage1("k")
@@ -353,6 +376,25 @@
         return 0
 
     lax.fori_loop(0, SLOTS, step_body, 0)
+
+    for copy in cache_loads:
+        copy.wait()
+
+    def c_store(slot):
+        return pltpu.make_async_copy(cbuf.at[slot % 2], part_hbm.at[slot], c_sem.at[slot % 2])
+
+    def cache_body(slot, _):
+        @pl.when(slot >= 2)
+        def _():
+            c_store(slot - 2).wait()
+
+        cache_products(cbuf, slot % 2, cw, shift, xbuf, slot)
+        c_store(slot).start()
+        return 0
+
+    lax.fori_loop(0, SLOTS, cache_body, 0)
+    for slot in range(SLOTS - 2, SLOTS):
+        c_store(slot).wait()
 
     for slot in range(ONLY):
         clip = only_clip(other_chip, core, slot)
@@ -376,14 +418,14 @@
         s_copy(link, tp).wait_send()
 
 
-def encode(x, weights, vectors):
+def encode(x, weights, vectors, cache_inputs):
     dma = pltpu.SemaphoreType.DMA
-    any_spec = pl.BlockSpec(memory_space=pl.ANY)
+    any_spec, vmem_spec = pl.BlockSpec(memory_space=pl.ANY), pl.BlockSpec(memory_space=pltpu.VMEM)
     return pl.pallas_call(
         encoder_kernel,
-        out_shape=jax.ShapeDtypeStruct((CLIPS, FRAMES, WIDTH), BF16),
-        in_specs=[any_spec] * 7 + [pl.BlockSpec(memory_space=pltpu.VMEM)] * 11,
-        out_specs=any_spec,
+        out_shape=(jax.ShapeDtypeStruct((CLIPS, FRAMES, WIDTH), BF16), jax.ShapeDtypeStruct((SLOTS, 2 * WIDTH, FRAMES), BF16)),
+        in_specs=[any_spec] * 7 + [vmem_spec] * 11 + [any_spec, any_spec, vmem_spec],
+        out_specs=(any_spec, any_spec),
         scratch_shapes=[
             pltpu.VMEM((8, WIDTH), F32), pltpu.VMEM((8, WIDTH), F32), pltpu.VMEM((8, HIDDEN), F32),
             pltpu.VMEM((SLOTS, FRAMES, WIDTH), BF16),
@@ -396,107 +438,138 @@
             pltpu.VMEM((FRAMES, 2 * WIDTH), BF16),
             pltpu.VMEM((SLOTS, FRAMES, WIDTH), F32),
             pltpu.VMEM((8, 2 * WIDTH), F32),
+            pltpu.VMEM((2 * WIDTH, WIDTH), BF16), pltpu.VMEM((WIDTH, 128), F32), pltpu.VMEM((2, 2 * WIDTH, FRAMES), BF16),
             dma((SLOTS, 3)), dma((SLOTS, 3)), dma((SLOTS,)),
             dma((8, 5)), dma((8, 5)), dma((8,)),
             dma((3,)), dma((3,)),
             dma((SLOTS + 2 * ONLY,)), dma((SLOTS + 2 * ONLY,)), dma((SLOTS,)),
+            dma((2, 4)), dma((2,)),
         ],
         compiler_params=pltpu.CompilerParams(collective_id=0, has_side_effects=True, vmem_limit_bytes=64 * 1024 * 1024 - 128 * 1024),
         name="encoder",
-    )(x, *weights, *vectors)
-
-
-def cache_kernel(e_hbm, wk_hbm, wv_hbm, bias_ref, k_hbm, v_hbm, enc_hbm, weights, shift, ebuf, obuf, w_sem, e_sem, out_sem, enc_sem):
+    )(x, *weights, *vectors, *cache_inputs)
+
+
+def cache_kernel(e_hbm, part_hbm, wk_hbm, wv_hbm, bias_ref, k_hbm, v_hbm, enc_hbm,
+                 weights, shift, ebuf, obuf, pbuf, encbuf, w_sem, e_sem, out_sem, enc_sem, p_sem, pout_sem, own_sem):
     tp = lax.axis_index("tp")
-
-    def load(clip):
-        return pltpu.make_async_copy(e_hbm.at[clip], ebuf.at[clip], e_sem.at[clip])
-
-    def stores(clip, slot):
+    chip, core = tp // 2, tp % 2
+    own_frames = pl.ds(pl.multiple_of(tp * LOC_FRAMES, LOC_FRAMES), LOC_FRAMES)
+
+    def other(index):
+        shared = (1 - core) * SHARED + index
+        only = 2 * SHARED + ((tp + 1 + (index - SHARED) // ONLY) % 4) * ONLY + (index - SHARED) % ONLY
+        return jnp.where(index < SHARED, shared, only)
+
+    def load(index):
+        return pltpu.make_async_copy(e_hbm.at[other(index)], ebuf.at[index], e_sem.at[index])
+
+    def stores(src, slot, clip, sems):
         copies = []
         for which, dst in enumerate((k_hbm, v_hbm)):
             for layer in range(4):
                 rows = pl.ds(which * WIDTH + layer * LOC_COLS, LOC_COLS)
-                copies.append(pltpu.make_async_copy(obuf.at[slot, rows, :], dst.at[layer, clip], out_sem.at[slot, which * 4 + layer]))
+                copies.append(pltpu.make_async_copy(src.at[slot, rows, :], dst.at[layer, clip], sems.at[slot, which * 4 + layer]))
         return copies
 
-    def enc_store(clip):
-        own = pl.ds(pl.multiple_of(tp * LOC_FRAMES, LOC_FRAMES), LOC_FRAMES)
-        return pltpu.make_async_copy(ebuf.at[clip, own, :], enc_hbm.at[clip], enc_sem.at[clip])
+    def enc_store(index):
+        return pltpu.make_async_copy(ebuf.at[index, own_frames, :], enc_hbm.at[other(index)], enc_sem.at[index])
+
+    def own_load(slot):
+        return pltpu.make_async_copy(e_hbm.at[clip_of(chip, core, slot), own_frames, :], encbuf.at[slot], own_sem.at[0, slot])
+
+    def own_store(slot):
+        return pltpu.make_async_copy(encbuf.at[slot], enc_hbm.at[clip_of(chip, core, slot)], own_sem.at[1, slot])
+
+    def part_load(slot):
+        return pltpu.make_async_copy(part_hbm.at[slot], pbuf.at[slot], p_sem.at[slot])
 
     load(0).start()
-    weight_loads = [pltpu.make_async_copy(src.at[layer], weights.at[pl.ds(which * WIDTH + layer * LOC_COLS, LOC_COLS), :], w_sem.at[which, layer])
-                    for which, src in enumerate((wk_hbm, wv_hbm)) for layer in range(4)]
+    weight_loads = cache_weight_loads(wk_hbm, wv_hbm, weights, w_sem)
     for copy in weight_loads:
         copy.start()
-    for clip in range(1, AHEAD):
-        load(clip).start()
-    rows = jnp.concatenate([bias_ref[...].astype(F32), jnp.zeros((4, LOC_COLS), F32)], axis=0)
-    for layer in range(4):
-        pick = (lax.broadcasted_iota(jnp.int32, (8, 128), 0) == layer).astype(F32)
-        shift[layer * LOC_COLS:(layer + 1) * LOC_COLS, :] = dot(rows, pick, TN)
+    for index in range(1, AHEAD):
+        load(index).start()
+    for slot in range(SLOTS):
+        part_load(slot).start()
+        own_load(slot).start()
+    lay_out_shift(bias_ref, shift)
     for copy in weight_loads:
         copy.wait()
 
+    def forward(slot):
+        part_load(slot).wait()
+        for copy in stores(pbuf, slot, clip_of(chip, core, slot), pout_sem):
+            copy.start()
+        own_load(slot).wait()
+        own_store(slot).start()
+
     def body(step, _):
         for half in range(2):
-            clip = 2 * step + half
-            slot = clip % OUT_SLOTS
-            load(clip).wait()
-            enc_store(clip).start()
-
-            @pl.when(clip + AHEAD < CLIPS)
+            index = 2 * step + half
+            load(index).wait()
+            enc_store(index).start()
+
+            @pl.when(index + AHEAD < OTHERS)
             def _():
-                load(clip + AHEAD).start()
-
-            @pl.when(clip >= OUT_SLOTS)
+                load(index + AHEAD).start()
+
+            @pl.when(index >= OUT_SLOTS)
             def _():
-                for copy in stores(clip - OUT_SLOTS, slot):
+                for copy in stores(obuf, index % OUT_SLOTS, other(index - OUT_SLOTS), out_sem):
                     copy.wait()
 
         for half in range(2):
-            clip = 2 * step + half
-            slot = clip % OUT_SLOTS
-            obuf[slot, 0:WIDTH, :] = dot(weights[0:WIDTH, :], ebuf[clip], NT).astype(BF16)
-            obuf[slot, WIDTH:2 * WIDTH, :] = (dot(weights[WIDTH:2 * WIDTH, :], ebuf[clip], NT) + jnp.concatenate([shift[...]] * 4, axis=1)).astype(BF16)
+            index = 2 * step + half
+            cache_products(obuf, index % OUT_SLOTS, weights, shift, ebuf, index)
         for half in range(2):
-            clip = 2 * step + half
-            for copy in stores(clip, clip % OUT_SLOTS):
+            index = 2 * step + half
+            for copy in stores(obuf, index % OUT_SLOTS, other(index), out_sem):
                 copy.start()
+        for slot in range(SLOTS):
+            @pl.when(step == min(slot, OTHERS // 2 - 1))
+            def _():
+                forward(slot)
         return 0
 
-    lax.fori_loop(0, CLIPS // 2, body, 0)
-    for clip in range(CLIPS - OUT_SLOTS, CLIPS):
-        for copy in stores(clip, clip % OUT_SLOTS):
+    lax.fori_loop(0, OTHERS // 2, body, 0)
+    for index in range(OTHERS - OUT_SLOTS, OTHERS):
+        for copy in stores(obuf, index % OUT_SLOTS, other(index), out_sem):
             copy.wait()
-    for clip in range(CLIPS):
-        enc_store(clip).wait()
-
-
-def caches(e_all, wck_t, wcv_t, bias):
+    for index in range(OTHERS):
+        enc_store(index).wait()
+    for slot in range(SLOTS):
+        own_store(slot).wait()
+        for copy in stores(pbuf, slot, clip_of(chip, core, slot), pout_sem):
+            copy.wait()
+
+
+def caches(e_all, part, cache_inputs):
     cache = jax.ShapeDtypeStruct((4, CLIPS, LOC_COLS, FRAMES), BF16)
     any_spec = pl.BlockSpec(memory_space=pl.ANY)
     dma = pltpu.SemaphoreType.DMA
     return pl.pallas_call(
         cache_kernel,
         out_shape=(cache, cache, jax.ShapeDtypeStruct((CLIPS, LOC_FRAMES, WIDTH), BF16)),
-        in_specs=[any_spec, any_spec, any_spec, pl.BlockSpec(memory_space=pltpu.VMEM)],
+        in_specs=[any_spec] * 4 + [pl.BlockSpec(memory_space=pltpu.VMEM)],
         out_specs=(any_spec, any_spec, any_spec),
         scratch_shapes=[
             pltpu.VMEM((2 * WIDTH, WIDTH), BF16), pltpu.VMEM((WIDTH, 128), F32),
-            pltpu.VMEM((CLIPS, FRAMES, WIDTH), BF16), pltpu.VMEM((OUT_SLOTS, 2 * WIDTH, FRAMES), BF16),
-            dma((2, 4)), dma((CLIPS,)), dma((OUT_SLOTS, 8)), dma((CLIPS,)),
+            pltpu.VMEM((OTHERS, FRAMES, WIDTH), BF16), pltpu.VMEM((OUT_SLOTS, 2 * WIDTH, FRAMES), BF16),
+            pltpu.VMEM((SLOTS, 2 * WIDTH, FRAMES), BF16), pltpu.VMEM((SLOTS, LOC_FRAMES, WIDTH), BF16),
+            dma((2, 4)), dma((OTHERS,)), dma((OUT_SLOTS, 8)), dma((OTHERS,)), dma((SLOTS,)), dma((SLOTS, 8)), dma((2, SLOTS)),
         ],
         compiler_params=pltpu.CompilerParams(vmem_limit_bytes=64 * 1024 * 1024 - 128 * 1024),
         name="caches",
-    )(e_all, wck_t, wcv_t, bias)
+    )(e_all, part, *cache_inputs)
 
 
 def device_body(hidden_loc, ln1_gain, ln1_bias, w_q, b_q, w_k, w_v, b_v, w_o, b_o, ln2_gain, ln2_bias, w_fc1, b_fc1, w_fc2, b_fc2, post_gain, post_bias, w_ck, w_cv, b_cv):
     weights = (w_q.T, w_k.T, w_v.T, w_o, w_fc1, w_fc2)
     vectors = (ln1_gain, ln1_bias, ln2_gain, ln2_bias, post_gain, post_bias, b_o, b_fc2, b_fc1, b_q, b_v)
-    e_all = encode(hidden_loc, weights, vectors)
-    k_t, v_t, enc_loc = caches(e_all, w_ck.transpose(0, 2, 1), w_cv.transpose(0, 2, 1), b_cv)
+    cache_inputs = (w_ck.transpose(0, 2, 1), w_cv.transpose(0, 2, 1), b_cv)
+    e_all, part = encode(hidden_loc, weights, vectors, cache_inputs)
+    k_t, v_t, enc_loc = caches(e_all, part, cache_inputs)
     shape = (4, CLIPS, FRAMES, 3, HEAD_DIM)
     return enc_loc, k_t.transpose(0, 1, 3, 2).reshape(shape), v_t.transpose(0, 1, 3, 2).reshape(shape)
 

time: 171 us -> 174 us (1.018)
  Pallas kernels: 171 us -> 173 us
    pallas_call x1, Pallas kernels: 143 us -> 150 us  [encode(): pl.pallas_call(encoder_kernel, out_shape=(jax.ShapeDtypeStruct((CLIPS, FR...]
    pallas_call x1, Pallas kernels: 27 us -> 23.5 us  [caches(): pl.pallas_call(cache_kernel, out_shape=(cache, cache, jax.ShapeDtypeStruc...]
where the time goes in v7:
time: 174 us
  Pallas kernels  173 us (99%)
    pallas_call x1, Pallas kernels, encode(): pl.pallas_call(encoder_kernel, out_shape=(jax.ShapeDtypeStruct((CLIPS, FR...  150 us
    pallas_call x1, Pallas kernels, caches(): pl.pallas_call(cache_kernel, out_shape=(cache, cache, jax.ShapeDtypeStruc...  23.5 us

profile of v7, /device:TPU:0, one launch (start us, length us, event | category | flops | bytes accessed | tf_op | source)
XLA Modules:
  0.0 174.1 jit_solution(11705697137531283566)
XLA Ops:
  0.6 149.9 %encoder.1 = (bf16[16,512,768]{2,1,0:T(8,128)(2,1)}, bf16[6,1536,512]{2,1,0:T(8,128)(2,1)}) custom-call(bf16[16,128,768]{2,1,0:T(8,128)(2,1)} %x_hbm.1, bf16[192,768]{1,0:T(8,128)(2,1)} %bitcast.15, bf16[192,768]{1,0:T(8,128)(2,1)} %bitcast.16, bf16[192,768]{1,0:T(8,128)(2,1)} %bitcast.17, bf16[192,768]{1,0:T(8,128)(2,1)} %wo_hbm.1, ...), custom_call_target="tpu_custom_call" | custom-call | tf_op jit(solution)/shard_map/encoder/pallas_call | solution.py:424
  150.6 23.5 %caches.1 = (bf16[4,16,192,512]{3,2,1,0:T(8,128)(2,1)}, bf16[4,16,192,512]{3,2,1,0:T(8,128)(2,1)}, bf16[16,128,768]{2,1,0:T(8,128)(2,1)}) custom-call(bf16[16,512,768]{2,1,0:T(8,128)(2,1)} %get-tuple-element.8.e_hbm, bf16[6,1536,512]{2,1,0:T(8,128)(2,1)} %get-tuple-element.9.part_hbm, bf16[4,192,768]{2,1,0:T(8,128)(2,1)} %bitcast.12, ...), custom_call_target="tpu_custom_call" | custom-call | tf_op jit(solution)/shard_map/caches/pallas_call | solution.py:551

commit v8 on v5

--- a/solution.py
+++ b/solution.py
@@ -19,15 +19,15 @@
 WIDE = (slice(0, 512), slice(512, 768))
 SHARED, ONLY = 4, 2
 SLOTS = SHARED + ONLY
-LAG = SLOTS // 2
+TURN = 4
 LN_ROWS = 64
 SEND_ORDER = ("q", "k", "v", 0, "o", 1, 2, "w1a", "w1b", 3, "w2a", "w2b", 4, 5)
 RELAYS = {
-    (0, 1): ((1, "o"),), (0, 5): ((2, "o"),),
-    (2, 2): ((1, "w1a"),), (2, 5): ((1, "w1b"), (2, "w1a")),
-    (3, 0): ((2, "w1b"),), (3, 3): ((1, "w2a"),), (3, 5): ((1, "w2b"), (2, "w2a")),
+    (0, 0): ((1, "o"),), (0, 2): ((2, "o"),),
+    (1, 3): ((1, "w1a"),), (2, 1): ((1, "w1b"),), (2, 3): ((2, "w1a"),),
+    (3, 0): ((2, "w1b"),), (3, 1): ((1, "w2a"),), (3, 3): ((1, "w2b"), (2, "w2a")),
 }
-OUT_SLOTS, AHEAD = 6, 4
+OUT_SLOTS, AHEAD = 6, 2
 
 NT = (((1,), (1,)), ((), ()))
 NN = (((1,), (0,)), ((), ()))
@@ -221,6 +221,14 @@
         for first in range(0, FRAMES, LN_ROWS):
             dst_store(first, norm_rows(src_load(first), gain, shift))
 
+    def relays(step, place):
+        for (when, where), todo in RELAYS.items():
+            if where == place:
+                @pl.when(step == when)
+                def _():
+                    for stage, name in todo:
+                        (w_stage1 if stage == 1 else w_stage2)(name)
+
     def attention(slot, step):
         x_wait(slot)
 
@@ -238,12 +246,6 @@
         keep = [(lane < 64).astype(F32).astype(BF16), (lane >= 64).astype(F32).astype(BF16)]
 
         def pair_body(pair, _):
-            for (when, where), todo in RELAYS.items():
-                @pl.when((step == when) & (pair == where))
-                def _():
-                    for stage, name in todo:
-                        (w_stage1 if stage == 1 else w_stage2)(name)
-
             cols = pl.ds(pl.multiple_of(pair * 128, 128), 128)
             keys_t = ktbuf[cols, :]
             values = qvbuf[:, pl.ds(pl.multiple_of(WIDTH + pair * 128, 128), 128)]
@@ -263,7 +265,11 @@
             obuf[:, cols] = jnp.where(lane < 64, outs[0], outs[1]).astype(BF16)
             return 0
 
-        lax.fori_loop(0, 6, pair_body, 0)
+        relays(step, 0)
+        lax.fori_loop(0, 3, pair_body, 0)
+        relays(step, 1)
+        lax.fori_loop(3, 6, pair_body, 0)
+        relays(step, 2)
 
         @pl.when(step == 0)
         def _():
@@ -324,33 +330,36 @@
 
     mlp_units = ("w1a", "w1b", "w2a", "w2b")
 
+    def far_body(slot, _):
+        mlp_far(slot)
+        return 0
+
     def step_body(step, _):
-        attention(step, step)
-
-        @pl.when(step == 0)
-        def _():
-            for name in mlp_units:
-                w_wait_near(name)
-
-        mlp_near(step)
-
-        @pl.when(step == LAG)
+        @pl.when(step == TURN)
         def _():
             w_stage2("w2b")
             for name in mlp_units:
                 w_wait_far(name)
 
-        @pl.when(step >= LAG)
+        @pl.when((step == TURN) | (step == SLOTS))
         def _():
-            def far_body(turn, _):
-                mlp_far(2 * (step - LAG) + turn)
-                return 0
-
-            lax.fori_loop(0, 2, far_body, 0)
+            lax.fori_loop(step - TURN, (step - TURN) * (SLOTS - ONLY) // (SLOTS - TURN) + ONLY, far_body, 0)
+
+        @pl.when(step < SLOTS)
+        def _():
+            attention(step, step)
+
+            @pl.when(step == 0)
+            def _():
+                for name in mlp_units:
+                    w_wait_near(name)
+
+            mlp_near(step)
+            relays(step, 3)
 
         return 0
 
-    lax.fori_loop(0, SLOTS, step_body, 0)
+    lax.fori_loop(0, SLOTS + 1, step_body, 0)
 
     for slot in range(ONLY):
         clip = only_clip(other_chip, core, slot)

time: 172 us -> 168 us (0.977)
  Pallas kernels: 171 us -> 167 us
    pallas_call x1, Pallas kernels: 144 us -> 140 us  [encode(): pl.pallas_call(encoder_kernel, out_shape=jax.ShapeDtypeStruct((CLIPS, FRA...]
where the time goes in v8:
time: 168 us
  Pallas kernels  167 us (99%)
    pallas_call x1, Pallas kernels, encode(): pl.pallas_call(encoder_kernel, out_shape=jax.ShapeDtypeStruct((CLIPS, FRA...  140 us
    pallas_call x1, Pallas kernels, caches(): pl.pallas_call(cache_kernel, out_shape=(cache, cache, jax.ShapeDtypeStruc...  26.8 us

profile of v8, /device:TPU:0, one launch (start us, length us, event | category | flops | bytes accessed | tf_op | source)
XLA Modules:
  0.0 167.9 jit_solution(2252102356401838984)
XLA Ops:
  0.6 140.4 %encoder.1.e_hbm = bf16[16,512,768]{2,1,0:T(8,128)(2,1)} custom-call(bf16[16,128,768]{2,1,0:T(8,128)(2,1)} %x_hbm.1, bf16[192,768]{1,0:T(8,128)(2,1)} %bitcast.13, bf16[192,768]{1,0:T(8,128)(2,1)} %bitcast.14, bf16[192,768]{1,0:T(8,128)(2,1)} %bitcast.15, bf16[192,768]{1,0:T(8,128)(2,1)} %wo_hbm.1, bf16[768,768]{1,0:T(8,128)(2,1)} %w1_hbm.1, ...), custom_call_target="tpu_custom_call" | custom-call | tf_op jit(solution)/shard_map/encoder/pallas_call | solution.py:389
  141.0 26.8 %caches.1 = (bf16[4,16,192,512]{3,2,1,0:T(8,128)(2,1)}, bf16[4,16,192,512]{3,2,1,0:T(8,128)(2,1)}, bf16[16,128,768]{2,1,0:T(8,128)(2,1)}) custom-call(bf16[16,512,768]{2,1,0:T(8,128)(2,1)} %encoder.1.e_hbm, bf16[4,192,768]{2,1,0:T(8,128)(2,1)} %bitcast.11, bf16[4,192,768]{2,1,0:T(8,128)(2,1)} %bitcast.12, bf16[4,192]{1,0:T(4,128)(2,1)} %bias_ref.1), custom_call_target="tpu_custom_call" | custom-call | tf_op jit(solution)/shard_map/caches/pallas_call | solution.py:487

commit v9 on v8

--- a/solution.py
+++ b/solution.py
@@ -19,13 +19,13 @@
 WIDE = (slice(0, 512), slice(512, 768))
 SHARED, ONLY = 4, 2
 SLOTS = SHARED + ONLY
-TURN = 4
+TURN = 5
 LN_ROWS = 64
-SEND_ORDER = ("q", "k", "v", 0, "o", 1, 2, "w1a", "w1b", 3, "w2a", "w2b", 4, 5)
+SEND_ORDER = ("q", "k", "v", 0, "o", 1, 2, "w1a", "w1b", 3, "w2a", 4, "w2b", "w2c", 5)
 RELAYS = {
     (0, 0): ((1, "o"),), (0, 2): ((2, "o"),),
     (1, 3): ((1, "w1a"),), (2, 1): ((1, "w1b"),), (2, 3): ((2, "w1a"),),
-    (3, 0): ((2, "w1b"),), (3, 1): ((1, "w2a"),), (3, 3): ((1, "w2b"), (2, "w2a")),
+    (3, 0): ((2, "w1b"),), (3, 3): ((1, "w2a"),), (4, 1): ((1, "w2b"),), (4, 2): ((1, "w2c"), (2, "w2a")), (4, 3): ((2, "w2b"),),
 }
 OUT_SLOTS, AHEAD = 6, 2
 
@@ -101,7 +101,8 @@
         "q": (0, wq_hbm, at_rows(wqv, 0), 0, 192), "k": (1, wk_hbm, at_rows(wk, 0), 0, 192),
         "v": (2, wv_hbm, at_rows(wqv, WIDTH), 0, 192), "o": (3, wo_hbm, at_rows(wo, 0), 0, 192),
         "w1a": (4, w1_hbm, at_columns, 0, 384), "w1b": (5, w1_hbm, at_columns, 384, 384),
-        "w2a": (6, w2_hbm, at_rows(w2, 0), 0, 384), "w2b": (7, w2_hbm, at_rows(w2, 0), 384, 384),
+        "w2a": (6, w2_hbm, at_rows(w2, 0), 0, 384), "w2b": (7, w2_hbm, at_rows(w2, 0), 384, 192),
+        "w2c": (8, w2_hbm, at_rows(w2, 0), 576, 192),
     }
 
     def w_local(name):
@@ -328,7 +329,7 @@
             e_local(slot, clip).start()
             e_sib(slot, clip).start()
 
-    mlp_units = ("w1a", "w1b", "w2a", "w2b")
+    mlp_units = ("w1a", "w1b", "w2a", "w2b", "w2c")
 
     def far_body(slot, _):
         mlp_far(slot)
@@ -337,13 +338,14 @@
     def step_body(step, _):
         @pl.when(step == TURN)
         def _():
-            w_stage2("w2b")
+            w_stage2("w2c")
             for name in mlp_units:
                 w_wait_far(name)
 
         @pl.when((step == TURN) | (step == SLOTS))
         def _():
-            lax.fori_loop(step - TURN, (step - TURN) * (SLOTS - ONLY) // (SLOTS - TURN) + ONLY, far_body, 0)
+            turn = (step - TURN) // (SLOTS - TURN)
+            lax.fori_loop(turn * ONLY, turn * (SLOTS - ONLY) + ONLY, far_body, 0)
 
         @pl.when(step < SLOTS)
         def _():
@@ -404,7 +406,7 @@
             pltpu.VMEM((SLOTS, FRAMES, WIDTH), F32),
             pltpu.VMEM((8, 2 * WIDTH), F32),
             dma((SLOTS, 3)), dma((SLOTS, 3)), dma((SLOTS,)),
-            dma((8, 5)), dma((8, 5)), dma((8,)),
+            dma((9, 5)), dma((9, 5)), dma((9,)),
             dma((3,)), dma((3,)),
             dma((SLOTS + 2 * ONLY,)), dma((SLOTS + 2 * ONLY,)), dma((SLOTS,)),
         ],

time: 168 us -> 166 us (0.988)
  Pallas kernels: 167 us -> 165 us
    pallas_call x1, Pallas kernels: 140 us -> 138 us  [encode(): pl.pallas_call(encoder_kernel, out_shape=jax.ShapeDtypeStruct((CLIPS, FRA...]
where the time goes in v9:
time: 166 us
  Pallas kernels  165 us (99%)
    pallas_call x1, Pallas kernels, encode(): pl.pallas_call(encoder_kernel, out_shape=jax.ShapeDtypeStruct((CLIPS, FRA...  138 us
    pallas_call x1, Pallas kernels, caches(): pl.pallas_call(cache_kernel, out_shape=(cache, cache, jax.ShapeDtypeStruc...  26.8 us

profile of v9, /device:TPU:0, one launch (start us, length us, event | category | flops | bytes accessed | tf_op | source)
XLA Modules:
  0.0 165.7 jit_solution(14412124815397386467)
XLA Ops:
  0.6 138.3 %encoder.1.e_hbm = bf16[16,512,768]{2,1,0:T(8,128)(2,1)} custom-call(bf16[16,128,768]{2,1,0:T(8,128)(2,1)} %x_hbm.1, bf16[192,768]{1,0:T(8,128)(2,1)} %bitcast.13, bf16[192,768]{1,0:T(8,128)(2,1)} %bitcast.14, bf16[192,768]{1,0:T(8,128)(2,1)} %bitcast.15, bf16[192,768]{1,0:T(8,128)(2,1)} %wo_hbm.1, bf16[768,768]{1,0:T(8,128)(2,1)} %w1_hbm.1, ...), custom_call_target="tpu_custom_call" | custom-call | tf_op jit(solution)/shard_map/encoder/pallas_call | solution.py:391
  138.9 26.8 %caches.1 = (bf16[4,16,192,512]{3,2,1,0:T(8,128)(2,1)}, bf16[4,16,192,512]{3,2,1,0:T(8,128)(2,1)}, bf16[16,128,768]{2,1,0:T(8,128)(2,1)}) custom-call(bf16[16,512,768]{2,1,0:T(8,128)(2,1)} %encoder.1.e_hbm, bf16[4,192,768]{2,1,0:T(8,128)(2,1)} %bitcast.11, bf16[4,192,768]{2,1,0:T(8,128)(2,1)} %bitcast.12, bf16[4,192]{1,0:T(4,128)(2,1)} %bias_ref.1), custom_call_target="tpu_custom_call" | custom-call | tf_op jit(solution)/shard_map/caches/pallas_call | solution.py:489
